TPU v7x, 256 devices: a whole 4x4x8 slice. The times are simulated.
256 devices in a mesh: grid: 8 (over z), orb: 16 (over y, x_hi, core), pts: 2 (over x_lo).
Axes of the slice: x: 4 (x_hi: 2, x_lo: 2; x = x_hi * 2 + x_lo), y: 4, z: 8, core: 2. Of those that a mesh axis runs over, the one named last changes fastest.
Arguments:
- orbitals: bfloat16 [2048, 2048], P('grid', 'orb'), may hold values from -6 to 6
- points: int32 [8192], replicated, may hold values from 0 to 2047
- fitting: bfloat16 [2048, 8192], P('grid', ('orb', 'pts')), may hold values from -0.0625 to 0.0625
- screened: bfloat16 [8192, 8192], P(('orb', 'pts'), 'grid'), may hold values from -0.0014648438 to 0.0014648438
Outputs:
- exchange_orbitals: float32 [2048, 2048], P(('orb', 'pts'), 'grid')
- exchange_matrix: float32 [2048, 2048], P(('orb', 'pts'), 'grid')
Inputs may be any that keep to these rules, and one draw needn't show every extreme that they name: Grid rows of the window; two points may name the same row.
All inputs are finite; a program needn't handle non-finite values.
Results may differ from a plain program's by a relative error of at most 0.005.
Values may be sent and summed in bfloat16 or wider, within the bound.
No kernel may reach another device: no remote copies, remote signals or barrier semaphores. Data moves between devices by JAX's collectives and lax.ppermute only.
A program may use at most 128 MiB of HBM per device.

v0:
```python
import math

import jax
import jax.numpy as jnp
from jax import lax
from jax.experimental import pallas as pl
from jax.experimental.pallas import tpu as pltpu
from jax.sharding import Mesh, PartitionSpec as P


BF = jnp.bfloat16
F32 = jnp.float32
ORB = ("y", "xh", "core")
PLANE = ("y", "xh", "core", "pts")
CHIPS = ("y", "xh", "pts")
X = ("xh", "pts")


def sent_to_all(x, axis):
    copies = jnp.broadcast_to(x, (lax.axis_size(axis), *x.shape))
    return lax.all_to_all(copies, axis, split_axis=0, concat_axis=0, tiled=True)


def from_next(x, step):
    n = lax.axis_size("y")
    return lax.ppermute(x, "y", [(i, (i - step) % n) for i in range(n)])


def with_twin(x):
    return lax.ppermute(x, X, [(0, 1), (1, 0), (2, 3), (3, 2)])


def with_mirror(x):
    return lax.ppermute(x, X, [(0, 3), (3, 0), (1, 2), (2, 1)])


def with_far(x):
    return lax.ppermute(x, X, [(0, 2), (2, 0), (1, 3), (3, 1)])


def along_y(first, second):
    after, before = from_next(first, 1), from_next(first, -1)
    after2, before2 = from_next(second, 1), from_next(second, -1)
    far = from_next(after, 1)
    far2 = from_next(before2, -1)
    return (first, after, far, before), (second, after2, far2, before2)


def along_x(first, second):
    twin, mirror = with_twin(first), with_mirror(first)
    twin2, mirror2 = with_twin(second), with_mirror(second)
    far = with_twin(mirror)
    far2 = with_mirror(twin2)
    return (first, twin, mirror, far), (second, twin2, mirror2, far2)


def other_core(x):
    return lax.ppermute(x, "core", [(0, 1), (1, 0)])


def pick_kernel(spots_ref, place_ref, *refs):
    pieces, (own_ref, other_ref, picked_out_ref, columns_out_ref) = refs[:16], refs[16:20]
    wide_ref, chosen_ref, rows_ref, picked_ref, columns_ref, sems = refs[20:]
    rows = own_ref.shape[0]
    rest = picked_ref.shape[0]
    height, width = pieces[0].shape[1:]
    alpha, beta = pieces[:8], pieces[8:]
    pts, y, xh = (place_ref[k] for k in range(3))
    part = height // 4
    group = 256

    for at in range(4):
        for col, roles in enumerate(((0, 1), (3, 2))):
            spot = 2 * lax.rem(y + at, 4) + (xh if col == 0 else 1 - xh)
            for k, role in enumerate(roles):
                half = pts if k == 0 else 1 - pts
                for low, (piece, which) in enumerate(
                    ((alpha[role + 4 * (at // 2)], at % 2), (beta[at + 4 * (role // 2)], role % 2))
                ):

                    def spread(i, _, piece=piece, which=which, low=low, spot=spot, half=half):
                        block = piece[which, pl.ds(pl.multiple_of(i * part, part), part), :]
                        row = pl.multiple_of((4 * low + i) * 2 * part + half * part, part)
                        columns_ref[spot, pl.ds(row, part), :] = block
                        wide_ref[pl.ds(row * 8 + spot, part, stride=8), :] = block.astype(F32)
                        return _

                    lax.fori_loop(0, 4, spread, 0)

    keep_columns = pltpu.make_async_copy(columns_ref, columns_out_ref, sems.at[0])
    keep_columns.start()

    def choose(i, _):
        for k in range(16):
            spot = pl.multiple_of(spots_ref[i * 16 + k] * 8, 8)
            to = pl.multiple_of(i * 128 + k * 8, 8)
            chosen_ref[pl.ds(to, 8), :] = wide_ref[pl.ds(spot, 8), :]
        return _

    lax.fori_loop(0, (2 * rows + rest) // 16, choose, 0)

    for target, first, count in ((picked_ref, 2 * rows, rest), (rows_ref, 0, 2 * rows)):
        for k in range(8):

            def gather(i, _, target=target, first=first, k=k):
                start = pl.multiple_of(i * group, group)
                block = chosen_ref[pl.ds((first + start) * 8 + k, group, stride=8), :]
                target[pl.ds(start, group), k * width : (k + 1) * width] = block.astype(BF)
                return _

            lax.fori_loop(0, count // group, gather, 0)

    keep_picked = pltpu.make_async_copy(picked_ref, picked_out_ref, sems.at[1])
    keep_picked.start()
    for k, out in enumerate((own_ref, other_ref)):
        out[...] = lax.dot_general(
            rows_ref[k * rows : (k + 1) * rows],
            picked_ref[...],
            (((1,), (1,)), ((), ())),
            preferred_element_type=F32,
        )
    keep_columns.wait()
    keep_picked.wait()


def pick(spots, place, pieces, rows):
    _, height, width = pieces[0].shape
    total, nrows = spots.shape[0], 4 * height
    rest = total - 2 * rows
    vm = pl.BlockSpec(memory_space=pltpu.VMEM)
    sm = pl.BlockSpec(memory_space=pltpu.SMEM)
    hbm = pl.BlockSpec(memory_space=pltpu.HBM)
    return pl.pallas_call(
        pick_kernel,
        in_specs=[sm, sm] + [vm] * 16,
        out_specs=[vm, vm, hbm, hbm],
        out_shape=[
            jax.ShapeDtypeStruct((rows, rest), F32),
            jax.ShapeDtypeStruct((rows, rest), F32),
            pltpu.HBM((rest, 8 * width), BF),
            pltpu.HBM((8, nrows, width), BF),
        ],
        scratch_shapes=[
            pltpu.VMEM((nrows * 8, width), F32),
            pltpu.VMEM((total * 8, width), F32),
            pltpu.VMEM((2 * rows, 8 * width), BF),
            pltpu.VMEM((rest, 8 * width), BF),
            pltpu.VMEM((8, nrows, width), BF),
            pltpu.SemaphoreType.DMA((2,)),
        ],
        compiler_params=pltpu.CompilerParams(vmem_limit_bytes=28 << 20),
        cost_estimate=pl.CostEstimate(
            flops=4 * rows * rest * 8 * width, bytes_accessed=32 * nrows * width, transcendentals=0
        ),
        name="pick",
    )(spots, place, *pieces)


def apply_kernel(place_ref, picked_ref, own_ref, other_ref, *refs):
    outs, held_ref = refs[:-1], refs[-1]
    rows = own_ref.shape[0]
    groups, n, share, _ = held_ref.shape
    for k, ref in enumerate((own_ref, other_ref)):
        product = jnp.dot(ref[...], picked_ref[...], preferred_element_type=F32)
        held_ref[:, :, :, k * rows : (k + 1) * rows] = product.T.reshape(groups, n, share, rows)
    for k, out in enumerate(outs[:n]):
        if k == n // 2:
            half = groups // 2
            spot = lax.rem(place_ref[0] + k, n)
            out[...] = held_ref[:half, spot].astype(BF)
            outs[n][...] = held_ref[half:, spot].astype(BF)
        else:
            out[...] = held_ref[:, lax.rem(place_ref[0] + k, n)].astype(BF)


def applied_shares(place, picked, own, other, n, share):
    rows, columns = own.shape[0], picked.shape[1]
    groups = columns // (n * share)
    vm = pl.BlockSpec(memory_space=pltpu.VMEM)
    counts = [groups] * n + [groups // 2]
    counts[n // 2] = groups // 2
    return pl.pallas_call(
        apply_kernel,
        in_specs=[pl.BlockSpec(memory_space=pltpu.SMEM)] + [vm] * 3,
        out_specs=[vm] * (n + 1),
        out_shape=[jax.ShapeDtypeStruct((c, share, 2 * rows), BF) for c in counts],
        scratch_shapes=[pltpu.VMEM((groups, n, share, 2 * rows), F32)],
        compiler_params=pltpu.CompilerParams(vmem_limit_bytes=16 << 20),
        cost_estimate=pl.CostEstimate(
            flops=4 * rows * columns * own.shape[1], bytes_accessed=8 * rows * columns, transcendentals=0
        ),
        name="applied",
    )(place, picked, own, other)


def to_grid(x, step):
    n = lax.axis_size("grid")
    return lax.ppermute(x, "grid", [(i, (i + step) % n) for i in range(n)])


def summed_on_grid(shares):
    total = shares[0].astype(F32)
    opposite = {1: shares[4], -1: shares[8]}
    near = {1: shares[1], -1: shares[7]}
    second = {1: shares[2], -1: shares[6]}
    third = {1: shares[3], -1: shares[5]}
    opposite = {way: to_grid(x, 3 * way) for way, x in opposite.items()}
    third = {way: to_grid(x, 2 * way) for way, x in third.items()}
    second = {way: to_grid(x, way) for way, x in second.items()}
    sums = []
    for way in (1, -1):
        none = jnp.zeros_like(opposite[way])
        both = [opposite[way], none] if way == 1 else [none, opposite[way]]
        terms = near[way], second[way], third[way], jnp.concatenate(both)
        sums.append(to_grid(sum(t.astype(F32) for t in terms).astype(BF), way))
    return (total + sums[0].astype(F32) + sums[1].astype(F32)).astype(BF)


def body(orbitals, points, fitting, screened):
    n_grid = lax.axis_size("grid")
    n_plane = lax.axis_size(PLANE)
    grid_index = lax.axis_index("grid")
    plane_index = lax.axis_index(PLANE)
    y, xh, core, pts = (lax.axis_index(a) for a in PLANE)
    rows_dev, width = orbitals.shape
    nrows = rows_dev * n_grid
    nfull = width * lax.axis_size(ORB)
    npoints = points.shape[0]
    row_block = npoints // n_plane
    column_block = npoints // n_grid
    share = nfull // (n_plane * n_grid)
    part = rows_dev // 2
    quarter = nrows // 4

    own_rows = lax.dynamic_slice_in_dim(orbitals, pts * part, part, 0)
    held = sent_to_all(own_rows, "grid").reshape(2, quarter, width)
    alpha, beta = held[0], held[1]
    alphas = [alpha, from_next(alpha, 1), from_next(alpha, 2), from_next(alpha, -1)]
    betas = [beta, with_twin(beta), with_mirror(beta), with_far(beta)]
    a_first, a_second = jnp.stack(alphas[:2]), jnp.stack(alphas[2:])
    b_first, b_second = jnp.stack(betas[:2]), jnp.stack(betas[2:])
    pieces = [x for part in along_x(a_first, a_second) + along_y(b_first, b_second) for x in part]

    copies = jnp.broadcast_to(fitting, (n_grid, *fitting.shape))
    fit_own = lax.all_to_all(copies, "grid", 0, 0, tiled=True).reshape(nrows, row_block)
    fit_other = other_core(fit_own)

    mine = lax.dynamic_slice_in_dim(points, plane_index * row_block, row_block, 0)
    theirs_index = plane_index + (1 - 2 * core) * lax.axis_size("pts")
    theirs = lax.dynamic_slice_in_dim(points, theirs_index * row_block, row_block, 0)
    block = lax.dynamic_slice_in_dim(points, grid_index * column_block, column_block, 0)
    wanted = jnp.concatenate([mine, theirs, block])
    place = jnp.stack([pts, y, xh])
    density, density_other, picked, columns = pick(wanted, place, pieces, row_block)

    density = density + other_core(density_other)
    masked = (density * screened.astype(F32)).astype(BF)
    masked_other = other_core(masked)
    masked_other, fit_own = lax.optimization_barrier((masked_other, fit_own))

    applied = summed_on_grid(
        applied_shares(grid_index[None], picked, masked, masked_other, n_grid, share)
    )
    applied = applied.reshape(-1, 2 * row_block)
    terms = sum(
        lax.dot_general(a, f, (((1,), (1,)), ((), ())), preferred_element_type=F32)
        for a, f in ((applied[:, :row_block], fit_own), (applied[:, row_block:], fit_other))
    ).astype(BF)
    parts = lax.all_to_all(terms.reshape(-1, share, nrows), CHIPS, 0, 0, tiled=True)
    exchange = -jnp.sum(parts.astype(F32), axis=0)
    exchange = jnp.stack([exchange, other_core(exchange)])
    exchange = jnp.where(core == 0, exchange, exchange[::-1])

    rounded = exchange.astype(BF).reshape(2 * share, nrows)
    matrix = lax.dot_general(
        rounded, columns, (((1,), (1,)), ((), ())), preferred_element_type=F32
    ) / math.sqrt(nrows)
    matrix = matrix.reshape(2, share, n_grid, width).transpose(2, 0, 1, 3)
    mine = exchange.reshape(2, share, n_grid, 2, width)
    mine = lax.dynamic_index_in_dim(mine, core, 3, keepdims=False).transpose(2, 0, 1, 3)
    both = jnp.stack([mine, matrix], axis=2).reshape(2 * n_grid, 2, share, width)
    both = lax.all_to_all(both, ("grid", "core"), 0, 0, tiled=True)
    both = both.reshape(n_grid, 2, 2, share, width).transpose(2, 0, 3, 1, 4)
    both = both.reshape(2, n_grid * share, 2 * width)
    return both[0], both[1]


def solution(mesh):
    n_grid, n_orb, n_pts = (mesh.shape[a] for a in ("grid", "orb", "pts"))
    fine = Mesh(
        mesh.devices.reshape(n_grid, n_orb // 4, 2, 2, n_pts),
        ("grid", "y", "xh", "core", "pts"),
    )
    in_specs = (P("grid", ORB), P(), P("grid", PLANE), P(PLANE, "grid"))
    out_specs = (P(PLANE, "grid"), P(PLANE, "grid"))
    return jax.shard_map(body, mesh=fine, in_specs=in_specs, out_specs=out_specs, check_vma=False)
```

profile of v0, /device:TPU:1, one launch (start us, length us, event | category | flops | bytes accessed | tf_op | source)
XLA Modules:
  0.0 186.0 jit_solution(11313279642861945640)
XLA Ops:
  0.6 0.8 copy-done
  1.5 19.3 %all_to_all.20 = bf16[8,128,128]{2,1,0:T(8,128)(2,1)S(1)} all-to-all(bf16[8,128,128]{2,1,0:T(8,128)(2,1)S(1)} %broadcast_in_dim.10), channel_id=1, replica_groups=mesh['grid'=8,'y'=4,'xh'=2,'core'=2,'pts'=2] {'grid'}, dimensions={0} | all-to-all | bytes 524288 | tf_op jit(solution)/shard_map/all_to_all | solution.py:21
  20.8 2.6 %collective-permute-start.13 = (bf16[512,128]{1,0:T(8,128)(2,1)S(1)}, bf16[512,128]{1,0:T(8,128)(2,1)S(1)}, u32[]{:S(2)}, u32[]{:S(2)}) collective-permute-start(bf16[512,128]{1,0:T(8,128)(2,1)S(1)} %bitcast.53), channel_id=1, source_target_pairs={{0,5},{5,0},{1,4},{4,1},{2,7},{7,2},{3,6},{6,3},{8,13},{13,8},{9,1... | collective-permute-start | bytes 393224 | tf_op jit(solution)/shard_map/ppermute | solution.py:34
  23.4 0.5 collective-permute-start.14
  23.9 2.9 %collective-permute-start.4 = (bf16[512,128]{1,0:T(8,128)(2,1)S(1)}, bf16[512,128]{1,0:T(8,128)(2,1)S(1)}, u32[]{:S(2)}, u32[]{:S(2)}) collective-permute-start(bf16[512,128]{1,0:T(8,128)(2,1)S(1)} %bitcast.49), channel_id=1, source_target_pairs={{0,16},{8,24},{16,0},{24,8},{1,17},{9,25},{17,1},{25,9},{2,18},{10... | collective-permute-start | bytes 393224 | tf_op jit(solution)/shard_map/ppermute | solution.py:26
  26.8 0.4 collective-permute-start.5
  27.2 0.3 collective-permute-start.9
  27.5 1.3 collective-permute-done.14
  28.9 1.4 collective-permute-start.16
  30.2 3.0 %collective-permute-done.5 = bf16[512,128]{1,0:T(8,128)(2,1)S(1)} collective-permute-done((bf16[512,128]{1,0:T(8,128)(2,1)S(1)}, bf16[512,128]{1,0:T(8,128)(2,1)S(1)}, u32[]{:S(2)}, u32[]{:S(2)}) %collective-permute-start.5) | collective-permute-done | bytes 131104 | tf_op jit(solution)/shard_map/ppermute | solution.py:26
  33.3 0.3 collective-permute-start.6
  33.7 2.5 %collective-permute-start.7 = (bf16[2,512,128]{2,1,0:T(8,128)(2,1)S(1)}, bf16[2,512,128]{2,1,0:T(8,128)(2,1)S(1)}, u32[]{:S(2)}, u32[]{:S(2)}) collective-permute-start(bf16[2,512,128]{2,1,0:T(8,128)(2,1)S(1)} %pad_maximum_fusion.1.refs_4_), channel_id=1, source_target_pairs={{0,5},{5,0},{1,4},{4,1},{2,7},{7,2},{3,6},{6,3},{8,13},{13,8},{9,1... | collective-permute-start | bytes 786440 | tf_op jit(solution)/shard_map/ppermute | solution.py:34
  36.3 1.2 collective-permute-done
  37.5 1.2 collective-permute-start.10
  38.7 2.6 %collective-permute-start.2 = (bf16[2,512,128]{2,1,0:T(8,128)(2,1)S(1)}, bf16[2,512,128]{2,1,0:T(8,128)(2,1)S(1)}, u32[]{:S(2)}, u32[]{:S(2)}) collective-permute-start(bf16[2,512,128]{2,1,0:T(8,128)(2,1)S(1)} %pad_maximum_fusion.refs_0_), channel_id=1, source_target_pairs={{0,5},{5,0},{1,4},{4,1},{2,7},{7,2},{3,6},{6,3},{8,13},{13,8},{9,1... | collective-permute-start | bytes 786440 | tf_op jit(solution)/shard_map/ppermute | solution.py:34
  41.3 0.5 collective-permute-start.12
  41.8 0.2 collective-permute-start.17
  42.0 3.3 %collective-permute-done.10.refs_9_ = bf16[2,512,128]{2,1,0:T(8,128)(2,1)S(1)} collective-permute-done((bf16[2,512,128]{2,1,0:T(8,128)(2,1)S(1)}, bf16[2,512,128]{2,1,0:T(8,128)(2,1)S(1)}, u32[]{:S(2)}, u32[]{:S(2)}) %collective-permute-start.10) | collective-permute-done | bytes 262176 | tf_op jit(solution)/shard_map/ppermute | solution.py:26
  45.3 2.5 %collective-permute-start.8 = (bf16[2,512,128]{2,1,0:T(8,128)(2,1)S(1)}, bf16[2,512,128]{2,1,0:T(8,128)(2,1)}, u32[]{:S(2)}, u32[]{:S(2)}) collective-permute-start(bf16[2,512,128]{2,1,0:T(8,128)(2,1)S(1)} %collective-permute-done.6.refs_5_), channel_id=1, source_target_pairs={{0,5},{5,0},{1,4},{4,1},{2,7},{7,2},{3,6},{6,3},{8,13},{13,8},{9,1... | collective-permute-start | bytes 786440 | tf_op jit(solution)/shard_map/ppermute | solution.py:34
  47.8 2.9 %collective-permute-start.11 = (bf16[2,512,128]{2,1,0:T(8,128)(2,1)S(1)}, bf16[2,512,128]{2,1,0:T(8,128)(2,1)}, u32[]{:S(2)}, u32[]{:S(2)}) collective-permute-start(bf16[2,512,128]{2,1,0:T(8,128)(2,1)S(1)} %collective-permute-done.10.refs_9_), channel_id=1, source_target_pairs={{0,24},{8,0},{16,8},{24,16},{1,25},{9,1},{17,9},{25,17},{2,26},{10... | collective-permute-start | bytes 786440 | tf_op jit(solution)/shard_map/ppermute | solution.py:26
  50.7 0.7 copy-done.3
  51.4 0.7 copy-done.1
  52.1 0.1 pad_add_fusion.1.place_ref
  52.2 0.7 dynamic_slice.18
  52.9 0.8 fusion.9
  53.8 0.7 copy-done.5
  54.5 0.7 copy-done.7
  55.2 3.3 %collective-permute-done.3.refs_3_ = bf16[2,512,128]{2,1,0:T(8,128)(2,1)S(1)} collective-permute-done((bf16[2,512,128]{2,1,0:T(8,128)(2,1)S(1)}, bf16[2,512,128]{2,1,0:T(8,128)(2,1)S(1)}, u32[]{:S(2)}, u32[]{:S(2)}) %collective-permute-start.3) | collective-permute-done | bytes 262176 | tf_op jit(solution)/shard_map/ppermute | solution.py:30
  58.4 0.7 copy-done.9
  59.1 0.9 copy-done.2
  60.1 0.9 copy-done.4
  61.0 0.9 copy-done.6
  62.0 0.9 copy-done.8
  62.9 0.9 copy-done.10
  63.9 10.9 %pick.1 = (f32[256,1024]{1,0:T(8,128)S(1)}, f32[256,1024]{1,0:T(8,128)}, bf16[1024,1024]{1,0:T(8,128)(2,1)}, bf16[8,2048,128]{2,1,0:T(8,128)(2,1)}) custom-call(s32[1536]{0:T(1024)S(1)} %pad_add_fusion.spots_ref, s32[3]{0:T(128)S(1)} %pad_add_fusion.1.place_ref, bf16[2,512,128]{2,1,0:T(8,128)(2,1)S(1)} %pad_maximum_fusion.refs_0_, ...), custom_call_target="tpu_custom_call" | custom-call | flops 1073741824 | bytes 8388608 | tf_op jit(solution)/shard_map/pick/pallas_call | solution.py:133
  74.8 4.8 %collective-permute-start.18 = (f32[256,1024]{1,0:T(8,128)}, f32[256,1024]{1,0:T(8,128)S(1)}, u32[]{:S(2)}, u32[]{:S(2)}) collective-permute-start(f32[256,1024]{1,0:T(8,128)} %get-tuple-element.19), channel_id=1, source_target_pairs={{0,2},{2,0},{1,3},{3,1},{4,6},{6,4},{5,7},{7,5},{8,10},{10,8},{9,1... | collective-permute-start | bytes 3145736 | tf_op jit(solution)/shard_map/ppermute | solution.py:58
  79.6 1.1 broadcast_in_dim.11
  80.7 3.6 %all-to-all-start.1 = ((bf16[8,256,256]{2,1,0:T(8,128)(2,1)}), bf16[8,256,256]{2,1,0:T(8,128)(2,1)S(1)}, u32[]{:S(2)}, u32[]{:S(2)}) async-start(bf16[8,256,256]{2,1,0:T(8,128)(2,1)} %broadcast_in_dim.11), calls=%async_computation.1 | async-start | bytes 2097152 | tf_op jit(solution)/shard_map/all_to_all | solution.py:245
  84.3 1.0 copy-done.12
  85.3 1.6 multiply_convert_fusion.own_ref
  86.9 0.2 collective-permute-start.19
  87.1 26.4 %all-to-all-done.1 = bf16[8,256,256]{2,1,0:T(8,128)(2,1)S(1)} async-done(((bf16[8,256,256]{2,1,0:T(8,128)(2,1)}), bf16[8,256,256]{2,1,0:T(8,128)(2,1)S(1)}, u32[]{:S(2)}, u32[]{:S(2)}) %all-to-all-start.1) | async-done | bytes 1048608 | tf_op jit(solution)/shard_map/all_to_all | solution.py:245
  113.5 0.5 collective-permute-start.28
  113.9 1.6 copy-done.11
  115.5 1.5 applied.1
  117.0 0.3 collective-permute-start.20
  117.4 2.3 %collective-permute-start.22 = (bf16[8,8,512]{2,1,0:T(8,128)(2,1)S(1)}, bf16[8,8,512]{2,1,0:T(8,128)(2,1)S(1)}, u32[]{:S(2)}, u32[]{:S(2)}) collective-permute-start(bf16[8,8,512]{2,1,0:T(8,128)(2,1)S(1)} %get-tuple-element.25), channel_id=1, source_target_pairs={{0,96},{32,128},{64,160},{96,192},{128,224},{160,0},{192,32},{224,... | collective-permute-start | bytes 196616 | tf_op jit(solution)/shard_map/ppermute | solution.py:198
  119.7 2.1 %collective-permute-start.24 = (bf16[16,8,512]{2,1,0:T(8,128)(2,1)S(1)}, bf16[16,8,512]{2,1,0:T(8,128)(2,1)S(1)}, u32[]{:S(2)}, u32[]{:S(2)}) collective-permute-start(bf16[16,8,512]{2,1,0:T(8,128)(2,1)S(1)} %get-tuple-element.27), channel_id=1, source_target_pairs={{0,224},{32,0},{64,32},{96,64},{128,96},{160,128},{192,160},{224,1... | collective-permute-start | bytes 393224 | tf_op jit(solution)/shard_map/ppermute | solution.py:198
  121.8 8.3 %collective-permute-done.22 = bf16[8,8,512]{2,1,0:T(8,128)(2,1)S(1)} collective-permute-done((bf16[8,8,512]{2,1,0:T(8,128)(2,1)S(1)}, bf16[8,8,512]{2,1,0:T(8,128)(2,1)S(1)}, u32[]{:S(2)}, u32[]{:S(2)}) %collective-permute-start.22) | collective-permute-done | bytes 65568 | tf_op jit(solution)/shard_map/ppermute | solution.py:198
  130.1 1.8 collective-permute-start.25
  132.0 3.5 %collective-permute-start.23 = (bf16[16,8,512]{2,1,0:T(8,128)(2,1)S(1)}, bf16[16,8,512]{2,1,0:T(8,128)(2,1)S(1)}, u32[]{:S(2)}, u32[]{:S(2)}) collective-permute-start(bf16[16,8,512]{2,1,0:T(8,128)(2,1)S(1)} %add_convert_fusion.2), channel_id=1, source_target_pairs={{0,32},{32,64},{64,96},{96,128},{128,160},{160,192},{192,224},{224... | collective-permute-start | bytes 393224 | tf_op jit(solution)/shard_map/ppermute | solution.py:198
  135.5 1.9 %collective-permute-done.26 = bf16[8,8,512]{2,1,0:T(8,128)(2,1)S(1)} collective-permute-done((bf16[8,8,512]{2,1,0:T(8,128)(2,1)S(1)}, bf16[8,8,512]{2,1,0:T(8,128)(2,1)S(1)}, u32[]{:S(2)}, u32[]{:S(2)}) %collective-permute-start.26) | collective-permute-done | bytes 65568 | tf_op jit(solution)/shard_map/ppermute | solution.py:198
  137.3 4.6 %collective-permute-done.25 = bf16[16,8,512]{2,1,0:T(8,128)(2,1)S(1)} collective-permute-done((bf16[16,8,512]{2,1,0:T(8,128)(2,1)S(1)}, bf16[16,8,512]{2,1,0:T(8,128)(2,1)S(1)}, u32[]{:S(2)}, u32[]{:S(2)}) %collective-permute-start.25) | collective-permute-done | bytes 131104 | tf_op jit(solution)/shard_map/ppermute | solution.py:198
  142.0 4.1 %collective-permute-start.27 = (bf16[16,8,512]{2,1,0:T(8,128)(2,1)S(1)}, bf16[16,8,512]{2,1,0:T(8,128)(2,1)S(1)}, u32[]{:S(2)}, u32[]{:S(2)}) collective-permute-start(bf16[16,8,512]{2,1,0:T(8,128)(2,1)S(1)} %add_convert_fusion.1), channel_id=1, source_target_pairs={{0,224},{32,0},{64,32},{96,64},{128,96},{160,128},{192,160},{224,1... | collective-permute-start | bytes 393224 | tf_op jit(solution)/shard_map/ppermute | solution.py:198
  146.1 4.4 %collective-permute-done.27 = bf16[16,8,512]{2,1,0:T(8,128)(2,1)S(1)} collective-permute-done((bf16[16,8,512]{2,1,0:T(8,128)(2,1)S(1)}, bf16[16,8,512]{2,1,0:T(8,128)(2,1)S(1)}, u32[]{:S(2)}, u32[]{:S(2)}) %collective-permute-start.27) | collective-permute-done | bytes 131104 | tf_op jit(solution)/shard_map/ppermute | solution.py:198
  150.6 0.5 fusion.3
  151.1 0.5 fusion.1
  151.6 15.6 %all_to_all.21 = bf16[16,8,2048]{2,1,0:T(8,128)(2,1)S(1)} all-to-all(bf16[16,8,2048]{2,1,0:T(8,128)(2,1)S(1)} %fusion.1), channel_id=1, replica_groups=mesh['grid'=8,'y'=4,'xh'=2,'core'=2,'pts'=2] {'y','xh','pts'}, dimensions={0} | all-to-all | bytes 1048576 | tf_op jit(solution)/shard_map/all_to_all | solution.py:269
  167.3 2.3 %collective-permute-start.29 = (f32[8,2048]{1,0:T(8,128)S(1)}, f32[8,2048]{1,0:T(8,128)S(1)}, u32[]{:S(2)}, u32[]{:S(2)}) collective-permute-start(f32[8,2048]{1,0:T(8,128)S(1)} %get-tuple-element.37), channel_id=1, source_target_pairs={{0,2},{2,0},{1,3},{3,1},{4,6},{6,4},{5,7},{7,5},{8,10},{10,8},{9,1... | collective-permute-start | bytes 196616 | tf_op jit(solution)/shard_map/ppermute | solution.py:58
  169.5 0.9 collective-permute-done.29
  170.5 0.1 reshape.51
  170.7 2.8 %convolution_multiply_fusion = f32[16,8,128]{2,0,1:T(8,128)S(1)} fusion(bf16[8,2048,128]{2,1,0:T(8,128)(2,1)} %get-tuple-element.31, f32[2,8,2048]{2,1,0:T(8,128)S(1)} %reverse_select_fusion), kind=kOutput, calls=%fused_computation.3 | convolution fusion | flops 67158016 | bytes 4390912 | tf_op jit(solution)/shard_map/dot_general | solution.py:275
  173.6 11.8 %all_to_all.22 = f32[16,2,8,128]{3,2,1,0:T(8,128)S(1)} all-to-all(f32[16,2,8,128]{3,2,1,0:T(8,128)S(1)} %copy.8), channel_id=1, replica_groups=mesh['grid'=8,'y'=4,'xh'=2,'core'=2,'pts'=2] {'grid','core'}, dimensions={0} | all-to-all | bytes 262144 | tf_op jit(solution)/shard_map/all_to_all | solution.py:282
  185.4 0.7 slice_bitcast_fusion
  (60 shorter events, 0.7 us)
Async XLA Ops:
  0.6 0.8 copy-start
  20.8 6.7 %collective-permute-start.13 = (bf16[512,128]{1,0:T(8,128)(2,1)S(1)}, bf16[512,128]{1,0:T(8,128)(2,1)S(1)}, u32[]{:S(2)}, u32[]{:S(2)}) collective-permute-start(bf16[512,128]{1,0:T(8,128)(2,1)S(1)} %bitcast.53), channel_id=1, source_target_pairs={{0,5},{5,0},{1,4},{4,1},{2,7},{7,2},{3,6},{6,3},{8,13},{13,8},{9,1... | collective-permute-start | bytes 393224 | tf_op jit(solution)/shard_map/ppermute | solution.py:34
  23.4 5.4 %collective-permute-start.14 = (bf16[512,128]{1,0:T(8,128)(2,1)S(1)}, bf16[512,128]{1,0:T(8,128)(2,1)S(1)}, u32[]{:S(2)}, u32[]{:S(2)}) collective-permute-start(bf16[512,128]{1,0:T(8,128)(2,1)S(1)} %bitcast.54), channel_id=1, source_target_pairs={{0,4},{4,0},{1,5},{5,1},{2,6},{6,2},{3,7},{7,3},{8,12},{12,8},{9,1... | collective-permute-start | bytes 393224 | tf_op jit(solution)/shard_map/ppermute | solution.py:38
  23.9 6.3 %collective-permute-start.4 = (bf16[512,128]{1,0:T(8,128)(2,1)S(1)}, bf16[512,128]{1,0:T(8,128)(2,1)S(1)}, u32[]{:S(2)}, u32[]{:S(2)}) collective-permute-start(bf16[512,128]{1,0:T(8,128)(2,1)S(1)} %bitcast.49), channel_id=1, source_target_pairs={{0,16},{8,24},{16,0},{24,8},{1,17},{9,25},{17,1},{25,9},{2,18},{10... | collective-permute-start | bytes 393224 | tf_op jit(solution)/shard_map/ppermute | solution.py:26
  26.8 6.4 %collective-permute-start.5 = (bf16[512,128]{1,0:T(8,128)(2,1)S(1)}, bf16[512,128]{1,0:T(8,128)(2,1)S(1)}, u32[]{:S(2)}, u32[]{:S(2)}) collective-permute-start(bf16[512,128]{1,0:T(8,128)(2,1)S(1)} %bitcast.50), channel_id=1, source_target_pairs={{0,8},{8,16},{16,24},{24,0},{1,9},{9,17},{17,25},{25,1},{2,10},{10... | collective-permute-start | bytes 393224 | tf_op jit(solution)/shard_map/ppermute | solution.py:26
  27.2 6.5 %collective-permute-start.9 = (bf16[512,128]{1,0:T(8,128)(2,1)S(1)}, bf16[512,128]{1,0:T(8,128)(2,1)S(1)}, u32[]{:S(2)}, u32[]{:S(2)}) collective-permute-start(bf16[512,128]{1,0:T(8,128)(2,1)S(1)} %bitcast.55), channel_id=1, source_target_pairs={{0,1},{1,0},{4,5},{5,4},{2,3},{3,2},{6,7},{7,6},{8,9},{9,8},{12,13... | collective-permute-start | bytes 393224 | tf_op jit(solution)/shard_map/ppermute | solution.py:30
  28.9 9.9 %collective-permute-start.16 = (bf16[2,512,128]{2,1,0:T(8,128)(2,1)S(1)}, bf16[2,512,128]{2,1,0:T(8,128)(2,1)S(1)}, u32[]{:S(2)}, u32[]{:S(2)}) collective-permute-start(bf16[2,512,128]{2,1,0:T(8,128)(2,1)S(1)} %pad_maximum_fusion.3.refs_12_), channel_id=1, source_target_pairs={{0,8},{8,16},{16,24},{24,0},{1,9},{9,17},{17,25},{25,1},{2,10},{10... | collective-permute-start | bytes 786440 | tf_op jit(solution)/shard_map/ppermute | solution.py:26
  33.3 8.0 %collective-permute-start.6 = (bf16[2,512,128]{2,1,0:T(8,128)(2,1)S(1)}, bf16[2,512,128]{2,1,0:T(8,128)(2,1)S(1)}, u32[]{:S(2)}, u32[]{:S(2)}) collective-permute-start(bf16[2,512,128]{2,1,0:T(8,128)(2,1)S(1)} %pad_maximum_fusion.1.refs_4_), channel_id=1, source_target_pairs={{0,1},{1,0},{4,5},{5,4},{2,3},{3,2},{6,7},{7,6},{8,9},{9,8},{12,13... | collective-permute-start | bytes 786440 | tf_op jit(solution)/shard_map/ppermute | solution.py:30
  33.6 3.8 %collective-permute-start = (bf16[512,128]{1,0:T(8,128)(2,1)S(1)}, bf16[512,128]{1,0:T(8,128)(2,1)S(1)}, u32[]{:S(2)}, u32[]{:S(2)}) collective-permute-start(bf16[512,128]{1,0:T(8,128)(2,1)S(1)} %bitcast.51), channel_id=1, source_target_pairs={{0,24},{8,0},{16,8},{24,16},{1,25},{9,1},{17,9},{25,17},{2,26},{10... | collective-permute-start | bytes 393224 | tf_op jit(solution)/shard_map/ppermute | solution.py:26
  33.6 8.2 %collective-permute-start.15 = (bf16[2,512,128]{2,1,0:T(8,128)(2,1)S(1)}, bf16[2,512,128]{2,1,0:T(8,128)(2,1)S(1)}, u32[]{:S(2)}, u32[]{:S(2)}) collective-permute-start(bf16[2,512,128]{2,1,0:T(8,128)(2,1)S(1)} %pad_maximum_fusion.3.refs_12_), channel_id=1, source_target_pairs={{0,24},{8,0},{16,8},{24,16},{1,25},{9,1},{17,9},{25,17},{2,26},{10... | collective-permute-start | bytes 786440 | tf_op jit(solution)/shard_map/ppermute | solution.py:26
  33.7 8.2 %collective-permute-start.7 = (bf16[2,512,128]{2,1,0:T(8,128)(2,1)S(1)}, bf16[2,512,128]{2,1,0:T(8,128)(2,1)S(1)}, u32[]{:S(2)}, u32[]{:S(2)}) collective-permute-start(bf16[2,512,128]{2,1,0:T(8,128)(2,1)S(1)} %pad_maximum_fusion.1.refs_4_), channel_id=1, source_target_pairs={{0,5},{5,0},{1,4},{4,1},{2,7},{7,2},{3,6},{6,3},{8,13},{13,8},{9,1... | collective-permute-start | bytes 786440 | tf_op jit(solution)/shard_map/ppermute | solution.py:34
  37.5 7.9 %collective-permute-start.10 = (bf16[2,512,128]{2,1,0:T(8,128)(2,1)S(1)}, bf16[2,512,128]{2,1,0:T(8,128)(2,1)S(1)}, u32[]{:S(2)}, u32[]{:S(2)}) collective-permute-start(bf16[2,512,128]{2,1,0:T(8,128)(2,1)S(1)} %pad_maximum_fusion.2.refs_8_), channel_id=1, source_target_pairs={{0,24},{8,0},{16,8},{24,16},{1,25},{9,1},{17,9},{25,17},{2,26},{10... | collective-permute-start | bytes 786440 | tf_op jit(solution)/shard_map/ppermute | solution.py:26
  38.7 9.1 %collective-permute-start.2 = (bf16[2,512,128]{2,1,0:T(8,128)(2,1)S(1)}, bf16[2,512,128]{2,1,0:T(8,128)(2,1)S(1)}, u32[]{:S(2)}, u32[]{:S(2)}) collective-permute-start(bf16[2,512,128]{2,1,0:T(8,128)(2,1)S(1)} %pad_maximum_fusion.refs_0_), channel_id=1, source_target_pairs={{0,5},{5,0},{1,4},{4,1},{2,7},{7,2},{3,6},{6,3},{8,13},{13,8},{9,1... | collective-permute-start | bytes 786440 | tf_op jit(solution)/shard_map/ppermute | solution.py:34
  41.3 9.4 %collective-permute-start.12 = (bf16[2,512,128]{2,1,0:T(8,128)(2,1)S(1)}, bf16[2,512,128]{2,1,0:T(8,128)(2,1)S(1)}, u32[]{:S(2)}, u32[]{:S(2)}) collective-permute-start(bf16[2,512,128]{2,1,0:T(8,128)(2,1)S(1)} %pad_maximum_fusion.2.refs_8_), channel_id=1, source_target_pairs={{0,8},{8,16},{16,24},{24,0},{1,9},{9,17},{17,25},{25,1},{2,10},{10... | collective-permute-start | bytes 786440 | tf_op jit(solution)/shard_map/ppermute | solution.py:26
  41.8 11.9 %collective-permute-start.1 = (bf16[2,512,128]{2,1,0:T(8,128)(2,1)S(1)}, bf16[2,512,128]{2,1,0:T(8,128)(2,1)S(1)}, u32[]{:S(2)}, u32[]{:S(2)}) collective-permute-start(bf16[2,512,128]{2,1,0:T(8,128)(2,1)S(1)} %pad_maximum_fusion.refs_0_), channel_id=1, source_target_pairs={{0,1},{1,0},{4,5},{5,4},{2,3},{3,2},{6,7},{7,6},{8,9},{9,8},{12,13... | collective-permute-start | bytes 786440 | tf_op jit(solution)/shard_map/ppermute | solution.py:30
  41.8 12.6 %collective-permute-start.17 = (bf16[2,512,128]{2,1,0:T(8,128)(2,1)S(1)}, bf16[2,512,128]{2,1,0:T(8,128)(2,1)S(1)}, u32[]{:S(2)}, u32[]{:S(2)}) collective-permute-start(bf16[2,512,128]{2,1,0:T(8,128)(2,1)S(1)} %collective-permute-done.16.refs_15_), channel_id=1, source_target_pairs={{0,8},{8,16},{16,24},{24,0},{1,9},{9,17},{17,25},{25,1},{2,10},{10... | collective-permute-start | bytes 786440 | tf_op jit(solution)/shard_map/ppermute | solution.py:26
  45.3 9.8 %collective-permute-start.8 = (bf16[2,512,128]{2,1,0:T(8,128)(2,1)S(1)}, bf16[2,512,128]{2,1,0:T(8,128)(2,1)}, u32[]{:S(2)}, u32[]{:S(2)}) collective-permute-start(bf16[2,512,128]{2,1,0:T(8,128)(2,1)S(1)} %collective-permute-done.6.refs_5_), channel_id=1, source_target_pairs={{0,5},{5,0},{1,4},{4,1},{2,7},{7,2},{3,6},{6,3},{8,13},{13,8},{9,1... | collective-permute-start | bytes 786440 | tf_op jit(solution)/shard_map/ppermute | solution.py:34
  47.8 7.4 %collective-permute-start.11 = (bf16[2,512,128]{2,1,0:T(8,128)(2,1)S(1)}, bf16[2,512,128]{2,1,0:T(8,128)(2,1)}, u32[]{:S(2)}, u32[]{:S(2)}) collective-permute-start(bf16[2,512,128]{2,1,0:T(8,128)(2,1)S(1)} %collective-permute-done.10.refs_9_), channel_id=1, source_target_pairs={{0,24},{8,0},{16,8},{24,16},{1,25},{9,1},{17,9},{25,17},{2,26},{10... | collective-permute-start | bytes 786440 | tf_op jit(solution)/shard_map/ppermute | solution.py:26
  50.7 0.7 copy-start.3
  51.4 7.0 %collective-permute-start.3 = (bf16[2,512,128]{2,1,0:T(8,128)(2,1)S(1)}, bf16[2,512,128]{2,1,0:T(8,128)(2,1)S(1)}, u32[]{:S(2)}, u32[]{:S(2)}) collective-permute-start(bf16[2,512,128]{2,1,0:T(8,128)(2,1)S(1)} %collective-permute-done.2.refs_2_), channel_id=1, source_target_pairs={{0,1},{1,0},{4,5},{5,4},{2,3},{3,2},{6,7},{7,6},{8,9},{9,8},{12,13... | collective-permute-start | bytes 786440 | tf_op jit(solution)/shard_map/ppermute | solution.py:30
  51.4 0.7 copy-start.1
  53.7 0.7 copy-start.5
  54.5 0.7 copy-start.7
  58.4 0.7 copy-start.9
  59.1 0.9 copy-start.2
  60.1 0.9 copy-start.4
  61.0 0.9 copy-start.6
  62.0 0.9 copy-start.8
  62.9 0.9 copy-start.10
  63.9 15.7 %copy-start.13 = (bf16[256,256]{1,0:T(8,128)(2,1)S(1)}, bf16[256,256]{1,0:T(8,128)(2,1)}, u32[]{:S(2)}) copy-start(bf16[256,256]{1,0:T(8,128)(2,1)} %param.6) | copy-start | bytes 393220
  74.8 9.5 %collective-permute-start.18 = (f32[256,1024]{1,0:T(8,128)}, f32[256,1024]{1,0:T(8,128)S(1)}, u32[]{:S(2)}, u32[]{:S(2)}) collective-permute-start(f32[256,1024]{1,0:T(8,128)} %get-tuple-element.19), channel_id=1, source_target_pairs={{0,2},{2,0},{1,3},{3,1},{4,6},{6,4},{5,7},{7,5},{8,10},{10,8},{9,1... | collective-permute-start | bytes 3145736 | tf_op jit(solution)/shard_map/ppermute | solution.py:58
  80.7 32.8 %all-to-all-start.1 = ((bf16[8,256,256]{2,1,0:T(8,128)(2,1)}), bf16[8,256,256]{2,1,0:T(8,128)(2,1)S(1)}, u32[]{:S(2)}, u32[]{:S(2)}) async-start(bf16[8,256,256]{2,1,0:T(8,128)(2,1)} %broadcast_in_dim.11), calls=%async_computation.1 | async-start | bytes 2097152 | tf_op jit(solution)/shard_map/all_to_all | solution.py:245
  84.3 1.0 copy-start.12
  86.9 27.0 %collective-permute-start.19 = (bf16[256,1024]{1,0:T(8,128)(2,1)S(1)}, bf16[256,1024]{1,0:T(8,128)(2,1)S(1)}, u32[]{:S(2)}, u32[]{:S(2)}) collective-permute-start(bf16[256,1024]{1,0:T(8,128)(2,1)S(1)} %multiply_convert_fusion.own_ref), channel_id=1, source_target_pairs={{0,2},{2,0},{1,3},{3,1},{4,6},{6,4},{5,7},{7,5},{8,10},{10,8},{9,1... | collective-permute-start | bytes 1572872 | tf_op jit(solution)/shard_map/ppermute | solution.py:58
  113.5 37.1 %collective-permute-start.28 = (bf16[2048,256]{1,0:T(8,128)(2,1)S(1)}, bf16[2048,256]{1,0:T(8,128)(2,1)S(1)}, u32[]{:S(2)}, u32[]{:S(2)}) collective-permute-start(bf16[2048,256]{1,0:T(8,128)(2,1)S(1)} %bitcast.46), channel_id=1, source_target_pairs={{0,2},{2,0},{1,3},{3,1},{4,6},{6,4},{5,7},{7,5},{8,10},{10,8},{9,1... | collective-permute-start | bytes 3145736 | tf_op jit(solution)/shard_map/ppermute | solution.py:58
  113.9 1.6 copy-start.11
  117.0 14.9 %collective-permute-start.20 = (bf16[16,8,512]{2,1,0:T(8,128)(2,1)S(1)}, bf16[16,8,512]{2,1,0:T(8,128)(2,1)S(1)}, u32[]{:S(2)}, u32[]{:S(2)}) collective-permute-start(bf16[16,8,512]{2,1,0:T(8,128)(2,1)S(1)} %get-tuple-element.23), channel_id=1, source_target_pairs={{0,32},{32,64},{64,96},{96,128},{128,160},{160,192},{192,224},{224... | collective-permute-start | bytes 393224 | tf_op jit(solution)/shard_map/ppermute | solution.py:198
  117.3 14.6 %collective-permute-start.21 = (bf16[16,8,512]{2,1,0:T(8,128)(2,1)S(1)}, bf16[16,8,512]{2,1,0:T(8,128)(2,1)S(1)}, u32[]{:S(2)}, u32[]{:S(2)}) collective-permute-start(bf16[16,8,512]{2,1,0:T(8,128)(2,1)S(1)} %get-tuple-element.24), channel_id=1, source_target_pairs={{0,64},{32,96},{64,128},{96,160},{128,192},{160,224},{192,0},{224,... | collective-permute-start | bytes 393224 | tf_op jit(solution)/shard_map/ppermute | solution.py:198
  117.4 12.7 %collective-permute-start.22 = (bf16[8,8,512]{2,1,0:T(8,128)(2,1)S(1)}, bf16[8,8,512]{2,1,0:T(8,128)(2,1)S(1)}, u32[]{:S(2)}, u32[]{:S(2)}) collective-permute-start(bf16[8,8,512]{2,1,0:T(8,128)(2,1)S(1)} %get-tuple-element.25), channel_id=1, source_target_pairs={{0,96},{32,128},{64,160},{96,192},{128,224},{160,0},{192,32},{224,... | collective-permute-start | bytes 196616 | tf_op jit(solution)/shard_map/ppermute | solution.py:198
  119.7 17.7 %collective-permute-start.24 = (bf16[16,8,512]{2,1,0:T(8,128)(2,1)S(1)}, bf16[16,8,512]{2,1,0:T(8,128)(2,1)S(1)}, u32[]{:S(2)}, u32[]{:S(2)}) collective-permute-start(bf16[16,8,512]{2,1,0:T(8,128)(2,1)S(1)} %get-tuple-element.27), channel_id=1, source_target_pairs={{0,224},{32,0},{64,32},{96,64},{128,96},{160,128},{192,160},{224,1... | collective-permute-start | bytes 393224 | tf_op jit(solution)/shard_map/ppermute | solution.py:198
  130.1 11.9 %collective-permute-start.25 = (bf16[16,8,512]{2,1,0:T(8,128)(2,1)S(1)}, bf16[16,8,512]{2,1,0:T(8,128)(2,1)S(1)}, u32[]{:S(2)}, u32[]{:S(2)}) collective-permute-start(bf16[16,8,512]{2,1,0:T(8,128)(2,1)S(1)} %get-tuple-element.28), channel_id=1, source_target_pairs={{0,192},{32,224},{64,0},{96,32},{128,64},{160,96},{192,128},{224,1... | collective-permute-start | bytes 393224 | tf_op jit(solution)/shard_map/ppermute | solution.py:198
  131.9 5.4 %collective-permute-start.26 = (bf16[8,8,512]{2,1,0:T(8,128)(2,1)S(1)}, bf16[8,8,512]{2,1,0:T(8,128)(2,1)S(1)}, u32[]{:S(2)}, u32[]{:S(2)}) collective-permute-start(bf16[8,8,512]{2,1,0:T(8,128)(2,1)S(1)} %get-tuple-element.29), channel_id=1, source_target_pairs={{0,160},{32,192},{64,224},{96,0},{128,32},{160,64},{192,96},{224,1... | collective-permute-start | bytes 196616 | tf_op jit(solution)/shard_map/ppermute | solution.py:198
  132.0 14.2 %collective-permute-start.23 = (bf16[16,8,512]{2,1,0:T(8,128)(2,1)S(1)}, bf16[16,8,512]{2,1,0:T(8,128)(2,1)S(1)}, u32[]{:S(2)}, u32[]{:S(2)}) collective-permute-start(bf16[16,8,512]{2,1,0:T(8,128)(2,1)S(1)} %add_convert_fusion.2), channel_id=1, source_target_pairs={{0,32},{32,64},{64,96},{96,128},{128,160},{160,192},{192,224},{224... | collective-permute-start | bytes 393224 | tf_op jit(solution)/shard_map/ppermute | solution.py:198
  142.0 8.5 %collective-permute-start.27 = (bf16[16,8,512]{2,1,0:T(8,128)(2,1)S(1)}, bf16[16,8,512]{2,1,0:T(8,128)(2,1)S(1)}, u32[]{:S(2)}, u32[]{:S(2)}) collective-permute-start(bf16[16,8,512]{2,1,0:T(8,128)(2,1)S(1)} %add_convert_fusion.1), channel_id=1, source_target_pairs={{0,224},{32,0},{64,32},{96,64},{128,96},{160,128},{192,160},{224,1... | collective-permute-start | bytes 393224 | tf_op jit(solution)/shard_map/ppermute | solution.py:198
  167.3 3.2 %collective-permute-start.29 = (f32[8,2048]{1,0:T(8,128)S(1)}, f32[8,2048]{1,0:T(8,128)S(1)}, u32[]{:S(2)}, u32[]{:S(2)}) collective-permute-start(f32[8,2048]{1,0:T(8,128)S(1)} %get-tuple-element.37), channel_id=1, source_target_pairs={{0,2},{2,0},{1,3},{3,1},{4,6},{6,4},{5,7},{7,5},{8,10},{10,8},{9,1... | collective-permute-start | bytes 196616 | tf_op jit(solution)/shard_map/ppermute | solution.py:58
where the time goes:
time: 187 us; the launch traced here: 186 us
  waiting for transfers between devices  58.7 us (31%)
  blocking collectives  46.7 us (25%)
  starting transfers between devices  46.2 us (25%)
  local copies, waits for them, and re-layouts  15.2 us (8%)
  Pallas kernels  12.4 us (7%)
  matrix products  3.79 us (2%)
  other arithmetic  2.13 us (1%)
    all_to_all x1, waiting for transfers between devices, body(): lax.all_to_all(copies, 'grid', 0, 0, tiled=True).reshape(nrows, row_block)  26.4 us
    all_to_all x1, blocking collectives, sent_to_all(): return lax.all_to_all(copies, axis, split_axis=0, concat_axis=0, tiled=True)  19.3 us
    ppermute x8, waiting for transfers between devices, to_grid(): return lax.ppermute(x, 'grid', [(i, (i + step) % n) for i in range(n)])  19.3 us
    all_to_all x1, blocking collectives, body(): lax.all_to_all(terms.reshape(-1, share, nrows), CHIPS, 0, 0, tiled=True)  15.6 us
    ppermute x8, starting transfers between devices, to_grid(): return lax.ppermute(x, 'grid', [(i, (i + step) % n) for i in range(n)])  14.1 us
    all_to_all x1, blocking collectives, body(): both = lax.all_to_all(both, ('grid', 'core'), 0, 0, tiled=True)  11.8 us
    unnamed x28, local copies, waits for them, and re-layouts  11.7 us
    pallas_call x1, Pallas kernels, pick(): pl.pallas_call(pick_kernel, in_specs=[sm, sm] + [vm] * 16, out_specs=[vm,...  10.9 us
  transfers between devices with their start and end apart: 31, of which 11 were waited for; matrix products, arithmetic and copies ran while one was open for 2% of the time, Pallas kernels for 1%

commit v1 on v0

--- a/solution.py
+++ b/solution.py
@@ -156,26 +156,45 @@
     )(spots, place, *pieces)
 
 
+def product_kernel(picked_ref, rows_ref, out_ref):
+    product = jnp.dot(rows_ref[...], picked_ref[...], preferred_element_type=F32)
+    out_ref[...] = product.T.reshape(out_ref.shape).astype(BF)
+
+
+def applied_rows(picked, rows, n, share):
+    count, columns = rows.shape[0], picked.shape[1]
+    vm = pl.BlockSpec(memory_space=pltpu.VMEM)
+    return pl.pallas_call(
+        product_kernel,
+        in_specs=[vm] * 2,
+        out_specs=vm,
+        out_shape=jax.ShapeDtypeStruct((columns // (n * share), n, share, count), BF),
+        compiler_params=pltpu.CompilerParams(vmem_limit_bytes=16 << 20),
+        cost_estimate=pl.CostEstimate(
+            flops=2 * count * columns * rows.shape[1], bytes_accessed=4 * count * columns, transcendentals=0
+        ),
+        name="own",
+    )(picked, rows)
+
+
 def apply_kernel(place_ref, picked_ref, own_ref, other_ref, *refs):
     outs, held_ref = refs[:-1], refs[-1]
-    rows = own_ref.shape[0]
-    groups, n, share, _ = held_ref.shape
-    for k, ref in enumerate((own_ref, other_ref)):
-        product = jnp.dot(ref[...], picked_ref[...], preferred_element_type=F32)
-        held_ref[:, :, :, k * rows : (k + 1) * rows] = product.T.reshape(groups, n, share, rows)
+    rows = other_ref.shape[0]
+    groups, n, _, _ = held_ref.shape
+    half = groups // 2
+    product = jnp.dot(other_ref[...], picked_ref[...], preferred_element_type=F32)
+    held_ref[...] = product.T.reshape(held_ref.shape)
     for k, out in enumerate(outs[:n]):
-        if k == n // 2:
-            half = groups // 2
-            spot = lax.rem(place_ref[0] + k, n)
-            out[...] = held_ref[:half, spot].astype(BF)
-            outs[n][...] = held_ref[half:, spot].astype(BF)
-        else:
-            out[...] = held_ref[:, lax.rem(place_ref[0] + k, n)].astype(BF)
-
-
-def applied_shares(place, picked, own, other, n, share):
-    rows, columns = own.shape[0], picked.shape[1]
-    groups = columns // (n * share)
+        spot = lax.rem(place_ref[0] + k, n)
+        split = [(out, 0, groups)] if k != n // 2 else [(out, 0, half), (outs[n], half, groups)]
+        for target, low, high in split:
+            target[:, :, :rows] = own_ref[low:high, spot]
+            target[:, :, rows:] = held_ref[low:high, spot].astype(BF)
+
+
+def applied_shares(place, picked, own, other):
+    groups, n, share, rows = own.shape
+    columns = picked.shape[1]
     vm = pl.BlockSpec(memory_space=pltpu.VMEM)
     counts = [groups] * n + [groups // 2]
     counts[n // 2] = groups // 2
@@ -184,10 +203,10 @@
         in_specs=[pl.BlockSpec(memory_space=pltpu.SMEM)] + [vm] * 3,
         out_specs=[vm] * (n + 1),
         out_shape=[jax.ShapeDtypeStruct((c, share, 2 * rows), BF) for c in counts],
-        scratch_shapes=[pltpu.VMEM((groups, n, share, 2 * rows), F32)],
+        scratch_shapes=[pltpu.VMEM((groups, n, share, rows), F32)],
         compiler_params=pltpu.CompilerParams(vmem_limit_bytes=16 << 20),
         cost_estimate=pl.CostEstimate(
-            flops=4 * rows * columns * own.shape[1], bytes_accessed=8 * rows * columns, transcendentals=0
+            flops=2 * rows * columns * other.shape[1], bytes_accessed=8 * rows * columns, transcendentals=0
         ),
         name="applied",
     )(place, picked, own, other)
@@ -256,10 +275,11 @@
     density = density + other_core(density_other)
     masked = (density * screened.astype(F32)).astype(BF)
     masked_other = other_core(masked)
+    applied_own = applied_rows(picked, masked, n_grid, share)
     masked_other, fit_own = lax.optimization_barrier((masked_other, fit_own))
 
     applied = summed_on_grid(
-        applied_shares(grid_index[None], picked, masked, masked_other, n_grid, share)
+        applied_shares(grid_index[None], picked, applied_own, masked_other)
     )
     applied = applied.reshape(-1, 2 * row_block)
     terms = sum(

time: 187 us -> 156 us (0.83)
  waiting for transfers between devices: 58.7 us -> 31.1 us
  local copies, waits for them, and re-layouts: 15.2 us -> 5.39 us
  starting transfers between devices: 46.2 us -> 52.2 us
  blocking collectives: 46.7 us -> 49 us
    all_to_all x1, waiting for transfers between devices: 26.4 us -> 0.01 us  [body(): lax.all_to_all(copies, 'grid', 0, 0, tiled=True).reshape(nrows, row_block)]
    unnamed x28 -> x6, local copies, waits for them, and re-layouts: 11.7 us -> 0.84 us
    ppermute x4, starting transfers between devices: 7.68 us -> 13.7 us  [other_core(): return lax.ppermute(x, 'core', [(0, 1), (1, 0)])]
    all_to_all x1, blocking collectives: 11.8 us -> 16.2 us  [body(): both = lax.all_to_all(both, ('grid', 'core'), 0, 0, tiled=True)]
    ppermute x4, waiting for transfers between devices: 3.26 us -> 0.01 us  [with_twin(): return lax.ppermute(x, X, [(0, 1), (1, 0), (2, 3), (3, 2)])]
    ppermute x4, waiting for transfers between devices: 0.91 us -> 3.8 us  [other_core(): return lax.ppermute(x, 'core', [(0, 1), (1, 0)])]
    all_to_all x1, blocking collectives: 15.6 us -> 13.6 us  [body(): lax.all_to_all(terms.reshape(-1, share, nrows), CHIPS, 0, 0, tiled=True)]
  transfers between devices with their start and end apart: 31 -> 31, of which waited for: 11 -> 10; matrix products, arithmetic and copies ran while one was open for 2% -> 3% of each run, Pallas kernels for 1% -> 7%
where the time goes in v1:
time: 156 us; the launch traced here: 155 us
  starting transfers between devices  52.2 us (33%)
  blocking collectives  49 us (31%)
  waiting for transfers between devices  31.1 us (20%)
  Pallas kernels  10.9 us (7%)
  local copies, waits for them, and re-layouts  5.39 us (3%)
  matrix products  5.01 us (3%)
    all_to_all x1, blocking collectives, sent_to_all(): return lax.all_to_all(copies, axis, split_axis=0, concat_axis=0, tiled=True)  19.3 us
    ppermute x8, waiting for transfers between devices, to_grid(): return lax.ppermute(x, 'grid', [(i, (i + step) % n) for i in range(n)])  18.5 us
    all_to_all x1, blocking collectives, body(): both = lax.all_to_all(both, ('grid', 'core'), 0, 0, tiled=True)  16.2 us
    ppermute x8, starting transfers between devices, to_grid(): return lax.ppermute(x, 'grid', [(i, (i + step) % n) for i in range(n)])  14.7 us
    ppermute x4, starting transfers between devices, other_core(): return lax.ppermute(x, 'core', [(0, 1), (1, 0)])  13.7 us
    all_to_all x1, blocking collectives, body(): lax.all_to_all(terms.reshape(-1, share, nrows), CHIPS, 0, 0, tiled=True)  13.6 us
    pallas_call x1, Pallas kernels, pick(): pl.pallas_call(pick_kernel, in_specs=[sm, sm] + [vm] * 16, out_specs=[vm,...  9.25 us
    ppermute x9, starting transfers between devices, from_next(): return lax.ppermute(x, 'y', [(i, (i - step) % n) for i in range(n)])  9.15 us
  transfers between devices with their start and end apart: 31, of which 10 were waited for; matrix products, arithmetic and copies ran while one was open for 3% of the time, Pallas kernels for 7%

profile of v1, /device:TPU:1, one launch (start us, length us, event | category | flops | bytes accessed | tf_op | source)
XLA Modules:
  0.0 155.3 jit_solution(11556050954622809216)
XLA Ops:
  0.6 0.0 copy-start
  0.6 0.8 copy-done
  1.5 19.3 %all_to_all.20 = bf16[8,128,128]{2,1,0:T(8,128)(2,1)S(1)} all-to-all(bf16[8,128,128]{2,1,0:T(8,128)(2,1)S(1)} %broadcast_in_dim.10), channel_id=1, replica_groups=mesh['grid'=8,'y'=4,'xh'=2,'core'=2,'pts'=2] {'grid'}, dimensions={0} | all-to-all | bytes 524288 | tf_op jit(solution)/shard_map/all_to_all | solution.py:21
  20.8 2.6 %collective-permute-start.13 = (bf16[512,128]{1,0:T(8,128)(2,1)S(1)}, bf16[512,128]{1,0:T(8,128)(2,1)S(1)}, u32[]{:S(2)}, u32[]{:S(2)}) collective-permute-start(bf16[512,128]{1,0:T(8,128)(2,1)S(1)} %bitcast.51), channel_id=1, source_target_pairs={{0,5},{5,0},{1,4},{4,1},{2,7},{7,2},{3,6},{6,3},{8,13},{13,8},{9,1... | collective-permute-start | bytes 393224 | tf_op jit(solution)/shard_map/ppermute | solution.py:34
  23.4 0.5 collective-permute-start.14
  23.9 2.9 %collective-permute-start.4 = (bf16[512,128]{1,0:T(8,128)(2,1)S(1)}, bf16[512,128]{1,0:T(8,128)(2,1)S(1)}, u32[]{:S(2)}, u32[]{:S(2)}) collective-permute-start(bf16[512,128]{1,0:T(8,128)(2,1)S(1)} %bitcast.47), channel_id=1, source_target_pairs={{0,16},{8,24},{16,0},{24,8},{1,17},{9,25},{17,1},{25,9},{2,18},{10... | collective-permute-start | bytes 393224 | tf_op jit(solution)/shard_map/ppermute | solution.py:26
  26.8 0.4 collective-permute-start.5
  27.2 0.3 collective-permute-start.9
  27.5 1.3 collective-permute-done.14
  28.9 1.4 collective-permute-start.16
  30.2 0.0 collective-permute-done.4
  30.2 3.0 %collective-permute-done.5 = bf16[512,128]{1,0:T(8,128)(2,1)S(1)} collective-permute-done((bf16[512,128]{1,0:T(8,128)(2,1)S(1)}, bf16[512,128]{1,0:T(8,128)(2,1)S(1)}, u32[]{:S(2)}, u32[]{:S(2)}) %collective-permute-start.5) | collective-permute-done | bytes 131104 | tf_op jit(solution)/shard_map/ppermute | solution.py:26
  33.3 0.3 collective-permute-start.6
  33.6 0.0 collective-permute-start
  33.6 0.0 collective-permute-start.15
  33.7 2.5 %collective-permute-start.7 = (bf16[2,512,128]{2,1,0:T(8,128)(2,1)S(1)}, bf16[2,512,128]{2,1,0:T(8,128)(2,1)S(1)}, u32[]{:S(2)}, u32[]{:S(2)}) collective-permute-start(bf16[2,512,128]{2,1,0:T(8,128)(2,1)S(1)} %pad_maximum_fusion.1.refs_4_), channel_id=1, source_target_pairs={{0,5},{5,0},{1,4},{4,1},{2,7},{7,2},{3,6},{6,3},{8,13},{13,8},{9,1... | collective-permute-start | bytes 786440 | tf_op jit(solution)/shard_map/ppermute | solution.py:34
  36.3 1.2 collective-permute-done
  37.5 1.2 collective-permute-start.10
  38.7 2.6 %collective-permute-start.2 = (bf16[2,512,128]{2,1,0:T(8,128)(2,1)S(1)}, bf16[2,512,128]{2,1,0:T(8,128)(2,1)S(1)}, u32[]{:S(2)}, u32[]{:S(2)}) collective-permute-start(bf16[2,512,128]{2,1,0:T(8,128)(2,1)S(1)} %pad_maximum_fusion.refs_0_), channel_id=1, source_target_pairs={{0,5},{5,0},{1,4},{4,1},{2,7},{7,2},{3,6},{6,3},{8,13},{13,8},{9,1... | collective-permute-start | bytes 786440 | tf_op jit(solution)/shard_map/ppermute | solution.py:34
  41.3 0.5 collective-permute-start.12
  41.8 2.0 %broadcast_in_dim.11 = bf16[8,256,256]{2,1,0:T(8,128)(2,1)} broadcast(bf16[256,256]{1,0:T(8,128)(2,1)} %param.6), dimensions={1,2} | broadcast | bytes 1179648 | tf_op jit(solution)/shard_map/broadcast_in_dim | solution.py:263
  43.9 4.2 %all-to-all-start.1 = ((bf16[8,256,256]{2,1,0:T(8,128)(2,1)}), bf16[8,256,256]{2,1,0:T(8,128)(2,1)}, u32[]{:S(2)}, u32[]{:S(2)}) async-start(bf16[8,256,256]{2,1,0:T(8,128)(2,1)} %broadcast_in_dim.11), calls=%async_computation.1 | async-start | bytes 2097152 | tf_op jit(solution)/shard_map/all_to_all | solution.py:264
  48.1 0.1 collective-permute-start.1
  48.3 0.1 collective-permute-start.17
  48.4 0.8 collective-permute-start.8
  49.1 2.6 %collective-permute-start.11 = (bf16[2,512,128]{2,1,0:T(8,128)(2,1)S(1)}, bf16[2,512,128]{2,1,0:T(8,128)(2,1)}, u32[]{:S(2)}, u32[]{:S(2)}) collective-permute-start(bf16[2,512,128]{2,1,0:T(8,128)(2,1)S(1)} %collective-permute-done.10.refs_9_), channel_id=1, source_target_pairs={{0,24},{8,0},{16,8},{24,16},{1,25},{9,1},{17,9},{25,17},{2,26},{10... | collective-permute-start | bytes 786440 | tf_op jit(solution)/shard_map/ppermute | solution.py:26
  51.7 0.7 collective-permute-start.3
  52.5 0.1 pad_add_fusion.1.place_ref
  52.6 0.7 dynamic_slice.18
  53.3 0.8 fusion.9
  54.2 3.1 %collective-permute-done.17.refs_14_ = bf16[2,512,128]{2,1,0:T(8,128)(2,1)S(1)} collective-permute-done((bf16[2,512,128]{2,1,0:T(8,128)(2,1)S(1)}, bf16[2,512,128]{2,1,0:T(8,128)(2,1)S(1)}, u32[]{:S(2)}, u32[]{:S(2)}) %collective-permute-start.17) | collective-permute-done | bytes 262176 | tf_op jit(solution)/shard_map/ppermute | solution.py:26
  57.3 9.3 %pick.1 = (f32[256,1024]{1,0:T(8,128)S(1)}, f32[256,1024]{1,0:T(8,128)S(1)}, bf16[1024,1024]{1,0:T(8,128)(2,1)}, bf16[8,2048,128]{2,1,0:T(8,128)(2,1)}) custom-call(s32[1536]{0:T(1024)S(1)} %pad_add_fusion.spots_ref, s32[3]{0:T(128)S(1)} %pad_add_fusion.1.place_ref, bf16[2,512,128]{2,1,0:T(8,128)(2,1)S(1)} %pad_maximum_fusion.refs_0_, ...), custom_call_target="tpu_custom_call" | custom-call | flops 1073741824 | bytes 8388608 | tf_op jit(solution)/shard_map/pick/pallas_call | solution.py:133
  66.6 9.8 %collective-permute-start.18 = (f32[256,1024]{1,0:T(8,128)S(1)}, f32[256,1024]{1,0:T(8,128)S(1)}, u32[]{:S(2)}, u32[]{:S(2)}) collective-permute-start(f32[256,1024]{1,0:T(8,128)S(1)} %get-tuple-element.19), channel_id=1, source_target_pairs={{0,2},{2,0},{1,3},{3,1},{4,6},{6,4},{5,7},{7,5},{8,10},{10,8},{9,1... | collective-permute-start | bytes 3145736 | tf_op jit(solution)/shard_map/ppermute | solution.py:58
  76.4 2.3 %collective-permute-done.18 = f32[256,1024]{1,0:T(8,128)S(1)} collective-permute-done((f32[256,1024]{1,0:T(8,128)S(1)}, f32[256,1024]{1,0:T(8,128)S(1)}, u32[]{:S(2)}, u32[]{:S(2)}) %collective-permute-start.18) | collective-permute-done | bytes 1048608 | tf_op jit(solution)/shard_map/ppermute | solution.py:58
  78.7 0.3 multiply_convert_fusion.rows_ref
  78.9 0.5 collective-permute-start.19
  79.4 0.1 collective-permute-start.28
  79.5 0.8 own.1.own_ref
  80.3 0.6 collective-permute-done.19.other_ref
  80.9 0.9 applied.1
  81.8 1.6 %collective-permute-start.20 = (bf16[16,8,512]{2,1,0:T(8,128)(2,1)S(1)}, bf16[16,8,512]{2,1,0:T(8,128)(2,1)S(1)}, u32[]{:S(2)}, u32[]{:S(2)}) collective-permute-start(bf16[16,8,512]{2,1,0:T(8,128)(2,1)S(1)} %get-tuple-element.23), channel_id=1, source_target_pairs={{0,32},{32,64},{64,96},{96,128},{128,160},{160,192},{192,224},{224... | collective-permute-start | bytes 393224 | tf_op jit(solution)/shard_map/ppermute | solution.py:217
  83.4 2.1 %collective-permute-start.21 = (bf16[16,8,512]{2,1,0:T(8,128)(2,1)S(1)}, bf16[16,8,512]{2,1,0:T(8,128)(2,1)S(1)}, u32[]{:S(2)}, u32[]{:S(2)}) collective-permute-start(bf16[16,8,512]{2,1,0:T(8,128)(2,1)S(1)} %get-tuple-element.24), channel_id=1, source_target_pairs={{0,64},{32,96},{64,128},{96,160},{128,192},{160,224},{192,0},{224,... | collective-permute-start | bytes 393224 | tf_op jit(solution)/shard_map/ppermute | solution.py:217
  85.5 2.4 %collective-permute-start.22 = (bf16[8,8,512]{2,1,0:T(8,128)(2,1)S(1)}, bf16[8,8,512]{2,1,0:T(8,128)(2,1)S(1)}, u32[]{:S(2)}, u32[]{:S(2)}) collective-permute-start(bf16[8,8,512]{2,1,0:T(8,128)(2,1)S(1)} %get-tuple-element.25), channel_id=1, source_target_pairs={{0,96},{32,128},{64,160},{96,192},{128,224},{160,0},{192,32},{224,... | collective-permute-start | bytes 196616 | tf_op jit(solution)/shard_map/ppermute | solution.py:217
  88.0 2.4 %collective-permute-start.24 = (bf16[16,8,512]{2,1,0:T(8,128)(2,1)S(1)}, bf16[16,8,512]{2,1,0:T(8,128)(2,1)S(1)}, u32[]{:S(2)}, u32[]{:S(2)}) collective-permute-start(bf16[16,8,512]{2,1,0:T(8,128)(2,1)S(1)} %get-tuple-element.27), channel_id=1, source_target_pairs={{0,224},{32,0},{64,32},{96,64},{128,96},{160,128},{192,160},{224,1... | collective-permute-start | bytes 393224 | tf_op jit(solution)/shard_map/ppermute | solution.py:217
  90.3 7.8 %collective-permute-done.22 = bf16[8,8,512]{2,1,0:T(8,128)(2,1)S(1)} collective-permute-done((bf16[8,8,512]{2,1,0:T(8,128)(2,1)S(1)}, bf16[8,8,512]{2,1,0:T(8,128)(2,1)S(1)}, u32[]{:S(2)}, u32[]{:S(2)}) %collective-permute-start.22) | collective-permute-done | bytes 65568 | tf_op jit(solution)/shard_map/ppermute | solution.py:217
  98.1 4.7 %collective-permute-start.25 = (bf16[16,8,512]{2,1,0:T(8,128)(2,1)S(1)}, bf16[16,8,512]{2,1,0:T(8,128)(2,1)S(1)}, u32[]{:S(2)}, u32[]{:S(2)}) collective-permute-start(bf16[16,8,512]{2,1,0:T(8,128)(2,1)S(1)} %get-tuple-element.28), channel_id=1, source_target_pairs={{0,192},{32,224},{64,0},{96,32},{128,64},{160,96},{192,128},{224,1... | collective-permute-start | bytes 393224 | tf_op jit(solution)/shard_map/ppermute | solution.py:217
  102.8 0.1 add_convert_fusion.2
  102.9 1.3 collective-permute-start.23
  104.1 7.0 %collective-permute-done.26 = bf16[8,8,512]{2,1,0:T(8,128)(2,1)S(1)} collective-permute-done((bf16[8,8,512]{2,1,0:T(8,128)(2,1)S(1)}, bf16[8,8,512]{2,1,0:T(8,128)(2,1)S(1)}, u32[]{:S(2)}, u32[]{:S(2)}) %collective-permute-start.26) | collective-permute-done | bytes 65568 | tf_op jit(solution)/shard_map/ppermute | solution.py:217
  111.1 0.1 add_convert_fusion.1
  111.2 0.3 collective-permute-start.27
  111.5 3.8 %collective-permute-done.27 = bf16[16,8,512]{2,1,0:T(8,128)(2,1)S(1)} collective-permute-done((bf16[16,8,512]{2,1,0:T(8,128)(2,1)S(1)}, bf16[16,8,512]{2,1,0:T(8,128)(2,1)S(1)}, u32[]{:S(2)}, u32[]{:S(2)}) %collective-permute-start.27) | collective-permute-done | bytes 131104 | tf_op jit(solution)/shard_map/ppermute | solution.py:217
  115.3 0.1 fusion.2
  115.3 0.5 fusion.3
  115.8 1.7 %fusion.1 = bf16[16,8,2048]{2,1,0:T(8,128)(2,1)S(1)} fusion(f32[128,2048]{1,0:T(8,128)S(1)} %fusion.3, bf16[2048,256]{1,0:T(8,128)(2,1)} %bitcast.14, bf16[128,512]{1,0:T(8,128)(2,1)S(1)} %fusion.2), kind=kOutput, calls=%fused_computation.2 | convolution fusion | flops 134742016 | bytes 2686976 | tf_op jit(solution)/shard_map/dot_general | solution.py:286
  117.5 13.6 %all_to_all.21 = bf16[16,8,2048]{2,1,0:T(8,128)(2,1)S(1)} all-to-all(bf16[16,8,2048]{2,1,0:T(8,128)(2,1)S(1)} %fusion.1), channel_id=1, replica_groups=mesh['grid'=8,'y'=4,'xh'=2,'core'=2,'pts'=2] {'y','xh','pts'}, dimensions={0} | all-to-all | bytes 1048576 | tf_op jit(solution)/shard_map/all_to_all | solution.py:289
  131.1 0.1 convert_reduce_fusion
  131.2 3.3 %collective-permute-start.29 = (f32[8,2048]{1,0:T(8,128)S(1)}, f32[8,2048]{1,0:T(8,128)S(1)}, u32[]{:S(2)}, u32[]{:S(2)}) collective-permute-start(f32[8,2048]{1,0:T(8,128)S(1)} %get-tuple-element.37), channel_id=1, source_target_pairs={{0,2},{2,0},{1,3},{3,1},{4,6},{6,4},{5,7},{7,5},{8,10},{10,8},{9,1... | collective-permute-start | bytes 196616 | tf_op jit(solution)/shard_map/ppermute | solution.py:58
  134.5 0.9 collective-permute-done.29
  135.4 0.1 reshape.51
  135.5 0.1 constant_dynamic-slice_fusion
  135.6 2.8 %convolution_multiply_fusion = f32[16,8,128]{2,0,1:T(8,128)S(1)} fusion(bf16[8,2048,128]{2,1,0:T(8,128)(2,1)} %get-tuple-element.31, f32[2,8,2048]{2,1,0:T(8,128)S(1)} %reverse_select_fusion), kind=kOutput, calls=%fused_computation.3 | convolution fusion | flops 67158016 | bytes 4390912 | tf_op jit(solution)/shard_map/dot_general | solution.py:295
  138.5 16.2 %all_to_all.22 = f32[16,2,8,128]{3,2,1,0:T(8,128)S(1)} all-to-all(f32[16,2,8,128]{3,2,1,0:T(8,128)S(1)} %copy.8), channel_id=1, replica_groups=mesh['grid'=8,'y'=4,'xh'=2,'core'=2,'pts'=2] {'grid','core'}, dimensions={0} | all-to-all | bytes 262144 | tf_op jit(solution)/shard_map/all_to_all | solution.py:302
  154.7 0.7 slice_bitcast_fusion
  (39 shorter events, 0.3 us)
Async XLA Ops:
  0.6 0.8 copy-start
  20.8 6.7 %collective-permute-start.13 = (bf16[512,128]{1,0:T(8,128)(2,1)S(1)}, bf16[512,128]{1,0:T(8,128)(2,1)S(1)}, u32[]{:S(2)}, u32[]{:S(2)}) collective-permute-start(bf16[512,128]{1,0:T(8,128)(2,1)S(1)} %bitcast.51), channel_id=1, source_target_pairs={{0,5},{5,0},{1,4},{4,1},{2,7},{7,2},{3,6},{6,3},{8,13},{13,8},{9,1... | collective-permute-start | bytes 393224 | tf_op jit(solution)/shard_map/ppermute | solution.py:34
  23.4 5.4 %collective-permute-start.14 = (bf16[512,128]{1,0:T(8,128)(2,1)S(1)}, bf16[512,128]{1,0:T(8,128)(2,1)S(1)}, u32[]{:S(2)}, u32[]{:S(2)}) collective-permute-start(bf16[512,128]{1,0:T(8,128)(2,1)S(1)} %bitcast.52), channel_id=1, source_target_pairs={{0,4},{4,0},{1,5},{5,1},{2,6},{6,2},{3,7},{7,3},{8,12},{12,8},{9,1... | collective-permute-start | bytes 393224 | tf_op jit(solution)/shard_map/ppermute | solution.py:38
  23.9 6.3 %collective-permute-start.4 = (bf16[512,128]{1,0:T(8,128)(2,1)S(1)}, bf16[512,128]{1,0:T(8,128)(2,1)S(1)}, u32[]{:S(2)}, u32[]{:S(2)}) collective-permute-start(bf16[512,128]{1,0:T(8,128)(2,1)S(1)} %bitcast.47), channel_id=1, source_target_pairs={{0,16},{8,24},{16,0},{24,8},{1,17},{9,25},{17,1},{25,9},{2,18},{10... | collective-permute-start | bytes 393224 | tf_op jit(solution)/shard_map/ppermute | solution.py:26
  26.8 6.4 %collective-permute-start.5 = (bf16[512,128]{1,0:T(8,128)(2,1)S(1)}, bf16[512,128]{1,0:T(8,128)(2,1)S(1)}, u32[]{:S(2)}, u32[]{:S(2)}) collective-permute-start(bf16[512,128]{1,0:T(8,128)(2,1)S(1)} %bitcast.48), channel_id=1, source_target_pairs={{0,8},{8,16},{16,24},{24,0},{1,9},{9,17},{17,25},{25,1},{2,10},{10... | collective-permute-start | bytes 393224 | tf_op jit(solution)/shard_map/ppermute | solution.py:26
  27.2 6.5 %collective-permute-start.9 = (bf16[512,128]{1,0:T(8,128)(2,1)S(1)}, bf16[512,128]{1,0:T(8,128)(2,1)S(1)}, u32[]{:S(2)}, u32[]{:S(2)}) collective-permute-start(bf16[512,128]{1,0:T(8,128)(2,1)S(1)} %bitcast.53), channel_id=1, source_target_pairs={{0,1},{1,0},{4,5},{5,4},{2,3},{3,2},{6,7},{7,6},{8,9},{9,8},{12,13... | collective-permute-start | bytes 393224 | tf_op jit(solution)/shard_map/ppermute | solution.py:30
  28.9 9.9 %collective-permute-start.16 = (bf16[2,512,128]{2,1,0:T(8,128)(2,1)S(1)}, bf16[2,512,128]{2,1,0:T(8,128)(2,1)S(1)}, u32[]{:S(2)}, u32[]{:S(2)}) collective-permute-start(bf16[2,512,128]{2,1,0:T(8,128)(2,1)S(1)} %pad_maximum_fusion.3.refs_12_), channel_id=1, source_target_pairs={{0,8},{8,16},{16,24},{24,0},{1,9},{9,17},{17,25},{25,1},{2,10},{10... | collective-permute-start | bytes 786440 | tf_op jit(solution)/shard_map/ppermute | solution.py:26
  33.3 8.0 %collective-permute-start.6 = (bf16[2,512,128]{2,1,0:T(8,128)(2,1)S(1)}, bf16[2,512,128]{2,1,0:T(8,128)(2,1)S(1)}, u32[]{:S(2)}, u32[]{:S(2)}) collective-permute-start(bf16[2,512,128]{2,1,0:T(8,128)(2,1)S(1)} %pad_maximum_fusion.1.refs_4_), channel_id=1, source_target_pairs={{0,1},{1,0},{4,5},{5,4},{2,3},{3,2},{6,7},{7,6},{8,9},{9,8},{12,13... | collective-permute-start | bytes 786440 | tf_op jit(solution)/shard_map/ppermute | solution.py:30
  33.6 3.8 %collective-permute-start = (bf16[512,128]{1,0:T(8,128)(2,1)S(1)}, bf16[512,128]{1,0:T(8,128)(2,1)S(1)}, u32[]{:S(2)}, u32[]{:S(2)}) collective-permute-start(bf16[512,128]{1,0:T(8,128)(2,1)S(1)} %bitcast.49), channel_id=1, source_target_pairs={{0,24},{8,0},{16,8},{24,16},{1,25},{9,1},{17,9},{25,17},{2,26},{10... | collective-permute-start | bytes 393224 | tf_op jit(solution)/shard_map/ppermute | solution.py:26
  33.6 14.5 %collective-permute-start.15 = (bf16[2,512,128]{2,1,0:T(8,128)(2,1)S(1)}, bf16[2,512,128]{2,1,0:T(8,128)(2,1)S(1)}, u32[]{:S(2)}, u32[]{:S(2)}) collective-permute-start(bf16[2,512,128]{2,1,0:T(8,128)(2,1)S(1)} %pad_maximum_fusion.3.refs_12_), channel_id=1, source_target_pairs={{0,24},{8,0},{16,8},{24,16},{1,25},{9,1},{17,9},{25,17},{2,26},{10... | collective-permute-start | bytes 786440 | tf_op jit(solution)/shard_map/ppermute | solution.py:26
  33.7 14.6 %collective-permute-start.7 = (bf16[2,512,128]{2,1,0:T(8,128)(2,1)S(1)}, bf16[2,512,128]{2,1,0:T(8,128)(2,1)S(1)}, u32[]{:S(2)}, u32[]{:S(2)}) collective-permute-start(bf16[2,512,128]{2,1,0:T(8,128)(2,1)S(1)} %pad_maximum_fusion.1.refs_4_), channel_id=1, source_target_pairs={{0,5},{5,0},{1,4},{4,1},{2,7},{7,2},{3,6},{6,3},{8,13},{13,8},{9,1... | collective-permute-start | bytes 786440 | tf_op jit(solution)/shard_map/ppermute | solution.py:34
  37.5 10.9 %collective-permute-start.10 = (bf16[2,512,128]{2,1,0:T(8,128)(2,1)S(1)}, bf16[2,512,128]{2,1,0:T(8,128)(2,1)S(1)}, u32[]{:S(2)}, u32[]{:S(2)}) collective-permute-start(bf16[2,512,128]{2,1,0:T(8,128)(2,1)S(1)} %pad_maximum_fusion.2.refs_8_), channel_id=1, source_target_pairs={{0,24},{8,0},{16,8},{24,16},{1,25},{9,1},{17,9},{25,17},{2,26},{10... | collective-permute-start | bytes 786440 | tf_op jit(solution)/shard_map/ppermute | solution.py:26
  38.7 10.4 %collective-permute-start.2 = (bf16[2,512,128]{2,1,0:T(8,128)(2,1)S(1)}, bf16[2,512,128]{2,1,0:T(8,128)(2,1)S(1)}, u32[]{:S(2)}, u32[]{:S(2)}) collective-permute-start(bf16[2,512,128]{2,1,0:T(8,128)(2,1)S(1)} %pad_maximum_fusion.refs_0_), channel_id=1, source_target_pairs={{0,5},{5,0},{1,4},{4,1},{2,7},{7,2},{3,6},{6,3},{8,13},{13,8},{9,1... | collective-permute-start | bytes 786440 | tf_op jit(solution)/shard_map/ppermute | solution.py:34
  41.3 10.4 %collective-permute-start.12 = (bf16[2,512,128]{2,1,0:T(8,128)(2,1)S(1)}, bf16[2,512,128]{2,1,0:T(8,128)(2,1)S(1)}, u32[]{:S(2)}, u32[]{:S(2)}) collective-permute-start(bf16[2,512,128]{2,1,0:T(8,128)(2,1)S(1)} %pad_maximum_fusion.2.refs_8_), channel_id=1, source_target_pairs={{0,8},{8,16},{16,24},{24,0},{1,9},{9,17},{17,25},{25,1},{2,10},{10... | collective-permute-start | bytes 786440 | tf_op jit(solution)/shard_map/ppermute | solution.py:26
  43.9 35.5 %all-to-all-start.1 = ((bf16[8,256,256]{2,1,0:T(8,128)(2,1)}), bf16[8,256,256]{2,1,0:T(8,128)(2,1)}, u32[]{:S(2)}, u32[]{:S(2)}) async-start(bf16[8,256,256]{2,1,0:T(8,128)(2,1)} %broadcast_in_dim.11), calls=%async_computation.1 | async-start | bytes 2097152 | tf_op jit(solution)/shard_map/all_to_all | solution.py:264
  48.1 6.0 %collective-permute-start.1 = (bf16[2,512,128]{2,1,0:T(8,128)(2,1)S(1)}, bf16[2,512,128]{2,1,0:T(8,128)(2,1)S(1)}, u32[]{:S(2)}, u32[]{:S(2)}) collective-permute-start(bf16[2,512,128]{2,1,0:T(8,128)(2,1)S(1)} %pad_maximum_fusion.refs_0_), channel_id=1, source_target_pairs={{0,1},{1,0},{4,5},{5,4},{2,3},{3,2},{6,7},{7,6},{8,9},{9,8},{12,13... | collective-permute-start | bytes 786440 | tf_op jit(solution)/shard_map/ppermute | solution.py:30
  48.3 9.0 %collective-permute-start.17 = (bf16[2,512,128]{2,1,0:T(8,128)(2,1)S(1)}, bf16[2,512,128]{2,1,0:T(8,128)(2,1)S(1)}, u32[]{:S(2)}, u32[]{:S(2)}) collective-permute-start(bf16[2,512,128]{2,1,0:T(8,128)(2,1)S(1)} %collective-permute-done.16.refs_15_), channel_id=1, source_target_pairs={{0,8},{8,16},{16,24},{24,0},{1,9},{9,17},{17,25},{25,1},{2,10},{10... | collective-permute-start | bytes 786440 | tf_op jit(solution)/shard_map/ppermute | solution.py:26
  48.4 8.9 %collective-permute-start.8 = (bf16[2,512,128]{2,1,0:T(8,128)(2,1)S(1)}, bf16[2,512,128]{2,1,0:T(8,128)(2,1)}, u32[]{:S(2)}, u32[]{:S(2)}) collective-permute-start(bf16[2,512,128]{2,1,0:T(8,128)(2,1)S(1)} %collective-permute-done.6.refs_5_), channel_id=1, source_target_pairs={{0,5},{5,0},{1,4},{4,1},{2,7},{7,2},{3,6},{6,3},{8,13},{13,8},{9,1... | collective-permute-start | bytes 786440 | tf_op jit(solution)/shard_map/ppermute | solution.py:34
  49.1 8.1 %collective-permute-start.11 = (bf16[2,512,128]{2,1,0:T(8,128)(2,1)S(1)}, bf16[2,512,128]{2,1,0:T(8,128)(2,1)}, u32[]{:S(2)}, u32[]{:S(2)}) collective-permute-start(bf16[2,512,128]{2,1,0:T(8,128)(2,1)S(1)} %collective-permute-done.10.refs_9_), channel_id=1, source_target_pairs={{0,24},{8,0},{16,8},{24,16},{1,25},{9,1},{17,9},{25,17},{2,26},{10... | collective-permute-start | bytes 786440 | tf_op jit(solution)/shard_map/ppermute | solution.py:26
  51.7 5.6 %collective-permute-start.3 = (bf16[2,512,128]{2,1,0:T(8,128)(2,1)S(1)}, bf16[2,512,128]{2,1,0:T(8,128)(2,1)}, u32[]{:S(2)}, u32[]{:S(2)}) collective-permute-start(bf16[2,512,128]{2,1,0:T(8,128)(2,1)S(1)} %collective-permute-done.2.refs_2_), channel_id=1, source_target_pairs={{0,1},{1,0},{4,5},{5,4},{2,3},{3,2},{6,7},{7,6},{8,9},{9,8},{12,13... | collective-permute-start | bytes 786440 | tf_op jit(solution)/shard_map/ppermute | solution.py:30
  52.5 26.1 %copy-start.2 = (bf16[256,1024]{1,0:T(8,128)(2,1)S(1)}, bf16[256,1024]{1,0:T(8,128)(2,1)}, u32[]{:S(2)}) copy-start(bf16[256,1024]{1,0:T(8,128)(2,1)} %param.7) | copy-start | bytes 1572868
  66.5 13.0 %copy-start.1 = (bf16[1024,1024]{1,0:T(8,128)(2,1)S(1)}, bf16[1024,1024]{1,0:T(8,128)(2,1)}, u32[]{:S(2)}) copy-start(bf16[1024,1024]{1,0:T(8,128)(2,1)} %get-tuple-element.17.picked_ref) | copy-start | bytes 6291460
  66.6 12.1 %collective-permute-start.18 = (f32[256,1024]{1,0:T(8,128)S(1)}, f32[256,1024]{1,0:T(8,128)S(1)}, u32[]{:S(2)}, u32[]{:S(2)}) collective-permute-start(f32[256,1024]{1,0:T(8,128)S(1)} %get-tuple-element.19), channel_id=1, source_target_pairs={{0,2},{2,0},{1,3},{3,1},{4,6},{6,4},{5,7},{7,5},{8,10},{10,8},{9,1... | collective-permute-start | bytes 3145736 | tf_op jit(solution)/shard_map/ppermute | solution.py:58
  78.9 2.0 %collective-permute-start.19 = (bf16[256,1024]{1,0:T(8,128)(2,1)S(1)}, bf16[256,1024]{1,0:T(8,128)(2,1)S(1)}, u32[]{:S(2)}, u32[]{:S(2)}) collective-permute-start(bf16[256,1024]{1,0:T(8,128)(2,1)S(1)} %multiply_convert_fusion.rows_ref), channel_id=1, source_target_pairs={{0,2},{2,0},{1,3},{3,1},{4,6},{6,4},{5,7},{7,5},{8,10},{10,8},{9,1... | collective-permute-start | bytes 1572872 | tf_op jit(solution)/shard_map/ppermute | solution.py:58
  79.4 35.9 %collective-permute-start.28 = (bf16[2048,256]{1,0:T(8,128)(2,1)}, bf16[2048,256]{1,0:T(8,128)(2,1)S(1)}, u32[]{:S(2)}, u32[]{:S(2)}) collective-permute-start(bf16[2048,256]{1,0:T(8,128)(2,1)} %bitcast.14), channel_id=1, source_target_pairs={{0,2},{2,0},{1,3},{3,1},{4,6},{6,4},{5,7},{7,5},{8,10},{10,8},{9,1... | collective-permute-start | bytes 3145736 | tf_op jit(solution)/shard_map/ppermute | solution.py:58
  81.8 21.0 %collective-permute-start.20 = (bf16[16,8,512]{2,1,0:T(8,128)(2,1)S(1)}, bf16[16,8,512]{2,1,0:T(8,128)(2,1)S(1)}, u32[]{:S(2)}, u32[]{:S(2)}) collective-permute-start(bf16[16,8,512]{2,1,0:T(8,128)(2,1)S(1)} %get-tuple-element.23), channel_id=1, source_target_pairs={{0,32},{32,64},{64,96},{96,128},{128,160},{160,192},{192,224},{224... | collective-permute-start | bytes 393224 | tf_op jit(solution)/shard_map/ppermute | solution.py:217
  83.4 19.4 %collective-permute-start.21 = (bf16[16,8,512]{2,1,0:T(8,128)(2,1)S(1)}, bf16[16,8,512]{2,1,0:T(8,128)(2,1)S(1)}, u32[]{:S(2)}, u32[]{:S(2)}) collective-permute-start(bf16[16,8,512]{2,1,0:T(8,128)(2,1)S(1)} %get-tuple-element.24), channel_id=1, source_target_pairs={{0,64},{32,96},{64,128},{96,160},{128,192},{160,224},{192,0},{224,... | collective-permute-start | bytes 393224 | tf_op jit(solution)/shard_map/ppermute | solution.py:217
  85.5 12.6 %collective-permute-start.22 = (bf16[8,8,512]{2,1,0:T(8,128)(2,1)S(1)}, bf16[8,8,512]{2,1,0:T(8,128)(2,1)S(1)}, u32[]{:S(2)}, u32[]{:S(2)}) collective-permute-start(bf16[8,8,512]{2,1,0:T(8,128)(2,1)S(1)} %get-tuple-element.25), channel_id=1, source_target_pairs={{0,96},{32,128},{64,160},{96,192},{128,224},{160,0},{192,32},{224,... | collective-permute-start | bytes 196616 | tf_op jit(solution)/shard_map/ppermute | solution.py:217
  88.0 23.1 %collective-permute-start.24 = (bf16[16,8,512]{2,1,0:T(8,128)(2,1)S(1)}, bf16[16,8,512]{2,1,0:T(8,128)(2,1)S(1)}, u32[]{:S(2)}, u32[]{:S(2)}) collective-permute-start(bf16[16,8,512]{2,1,0:T(8,128)(2,1)S(1)} %get-tuple-element.27), channel_id=1, source_target_pairs={{0,224},{32,0},{64,32},{96,64},{128,96},{160,128},{192,160},{224,1... | collective-permute-start | bytes 393224 | tf_op jit(solution)/shard_map/ppermute | solution.py:217
  98.1 13.0 %collective-permute-start.25 = (bf16[16,8,512]{2,1,0:T(8,128)(2,1)S(1)}, bf16[16,8,512]{2,1,0:T(8,128)(2,1)S(1)}, u32[]{:S(2)}, u32[]{:S(2)}) collective-permute-start(bf16[16,8,512]{2,1,0:T(8,128)(2,1)S(1)} %get-tuple-element.28), channel_id=1, source_target_pairs={{0,192},{32,224},{64,0},{96,32},{128,64},{160,96},{192,128},{224,1... | collective-permute-start | bytes 393224 | tf_op jit(solution)/shard_map/ppermute | solution.py:217
  102.8 8.3 %collective-permute-start.26 = (bf16[8,8,512]{2,1,0:T(8,128)(2,1)S(1)}, bf16[8,8,512]{2,1,0:T(8,128)(2,1)S(1)}, u32[]{:S(2)}, u32[]{:S(2)}) collective-permute-start(bf16[8,8,512]{2,1,0:T(8,128)(2,1)S(1)} %get-tuple-element.29), channel_id=1, source_target_pairs={{0,160},{32,192},{64,224},{96,0},{128,32},{160,64},{192,96},{224,1... | collective-permute-start | bytes 196616 | tf_op jit(solution)/shard_map/ppermute | solution.py:217
  102.9 8.6 %collective-permute-start.23 = (bf16[16,8,512]{2,1,0:T(8,128)(2,1)S(1)}, bf16[16,8,512]{2,1,0:T(8,128)(2,1)S(1)}, u32[]{:S(2)}, u32[]{:S(2)}) collective-permute-start(bf16[16,8,512]{2,1,0:T(8,128)(2,1)S(1)} %add_convert_fusion.2), channel_id=1, source_target_pairs={{0,32},{32,64},{64,96},{96,128},{128,160},{160,192},{192,224},{224... | collective-permute-start | bytes 393224 | tf_op jit(solution)/shard_map/ppermute | solution.py:217
  111.2 4.1 %collective-permute-start.27 = (bf16[16,8,512]{2,1,0:T(8,128)(2,1)S(1)}, bf16[16,8,512]{2,1,0:T(8,128)(2,1)S(1)}, u32[]{:S(2)}, u32[]{:S(2)}) collective-permute-start(bf16[16,8,512]{2,1,0:T(8,128)(2,1)S(1)} %add_convert_fusion.1), channel_id=1, source_target_pairs={{0,224},{32,0},{64,32},{96,64},{128,96},{160,128},{192,160},{224,1... | collective-permute-start | bytes 393224 | tf_op jit(solution)/shard_map/ppermute | solution.py:217
  131.2 4.2 %collective-permute-start.29 = (f32[8,2048]{1,0:T(8,128)S(1)}, f32[8,2048]{1,0:T(8,128)S(1)}, u32[]{:S(2)}, u32[]{:S(2)}) collective-permute-start(f32[8,2048]{1,0:T(8,128)S(1)} %get-tuple-element.37), channel_id=1, source_target_pairs={{0,2},{2,0},{1,3},{3,1},{4,6},{6,4},{5,7},{7,5},{8,10},{10,8},{9,1... | collective-permute-start | bytes 196616 | tf_op jit(solution)/shard_map/ppermute | solution.py:58

commit v2 on v1

--- a/solution.py
+++ b/solution.py
@@ -67,7 +67,7 @@
     alpha, beta = pieces[:8], pieces[8:]
     pts, y, xh = (place_ref[k] for k in range(3))
     part = height // 4
-    group = 256
+    group = 512
 
     for at in range(4):
         for col, roles in enumerate(((0, 1), (3, 2))):
@@ -79,25 +79,26 @@
                 ):
 
                     def spread(i, _, piece=piece, which=which, low=low, spot=spot, half=half):
-                        block = piece[which, pl.ds(pl.multiple_of(i * part, part), part), :]
-                        row = pl.multiple_of((4 * low + i) * 2 * part + half * part, part)
-                        columns_ref[spot, pl.ds(row, part), :] = block
-                        wide_ref[pl.ds(row * 8 + spot, part, stride=8), :] = block.astype(F32)
+                        for step in (2 * i, 2 * i + 1):
+                            block = piece[which, pl.ds(pl.multiple_of(step * part, part), part), :]
+                            row = pl.multiple_of((4 * low + step) * 2 * part + half * part, part)
+                            columns_ref[spot, pl.ds(row, part), :] = block
+                            wide_ref[pl.ds(row * 8 + spot, part, stride=8), :] = block.astype(F32)
                         return _
 
-                    lax.fori_loop(0, 4, spread, 0)
+                    lax.fori_loop(0, 2, spread, 0)
 
     keep_columns = pltpu.make_async_copy(columns_ref, columns_out_ref, sems.at[0])
     keep_columns.start()
 
     def choose(i, _):
-        for k in range(16):
-            spot = pl.multiple_of(spots_ref[i * 16 + k] * 8, 8)
-            to = pl.multiple_of(i * 128 + k * 8, 8)
+        for k in range(32):
+            spot = pl.multiple_of(spots_ref[i * 32 + k] * 8, 8)
+            to = pl.multiple_of(i * 256 + k * 8, 8)
             chosen_ref[pl.ds(to, 8), :] = wide_ref[pl.ds(spot, 8), :]
         return _
 
-    lax.fori_loop(0, (2 * rows + rest) // 16, choose, 0)
+    lax.fori_loop(0, (2 * rows + rest) // 32, choose, 0)
 
     for target, first, count in ((picked_ref, 2 * rows, rest), (rows_ref, 0, 2 * rows)):
         for k in range(8):

time: 156 us -> 155 us (level)
  transfers between devices with their start and end apart: 31 -> 31, of which waited for: 10 -> 10; matrix products, arithmetic and copies ran while one was open for 3% -> 3% of each run, Pallas kernels for 7% -> 6%
where the time goes in v2:
time: 155 us; the launch traced here: 154 us
  starting transfers between devices  52.2 us (34%)
  blocking collectives  49.1 us (32%)
  waiting for transfers between devices  31.1 us (20%)
  Pallas kernels  9.96 us (6%)
  local copies, waits for them, and re-layouts  5.39 us (3%)
  matrix products  5.01 us (3%)
    all_to_all x1, blocking collectives, sent_to_all(): return lax.all_to_all(copies, axis, split_axis=0, concat_axis=0, tiled=True)  19.3 us
    ppermute x8, waiting for transfers between devices, to_grid(): return lax.ppermute(x, 'grid', [(i, (i + step) % n) for i in range(n)])  18.5 us
    all_to_all x1, blocking collectives, body(): both = lax.all_to_all(both, ('grid', 'core'), 0, 0, tiled=True)  16.2 us
    ppermute x8, starting transfers between devices, to_grid(): return lax.ppermute(x, 'grid', [(i, (i + step) % n) for i in range(n)])  14.7 us
    ppermute x4, starting transfers between devices, other_core(): return lax.ppermute(x, 'core', [(0, 1), (1, 0)])  13.7 us
    all_to_all x1, blocking collectives, body(): lax.all_to_all(terms.reshape(-1, share, nrows), CHIPS, 0, 0, tiled=True)  13.6 us
    ppermute x9, starting transfers between devices, from_next(): return lax.ppermute(x, 'y', [(i, (i - step) % n) for i in range(n)])  9.15 us
    ppermute x4, starting transfers between devices, with_mirror(): return lax.ppermute(x, X, [(0, 3), (3, 0), (1, 2), (2, 1)])  8.44 us
  transfers between devices with their start and end apart: 31, of which 10 were waited for; matrix products, arithmetic and copies ran while one was open for 3% of the time, Pallas kernels for 6%

profile of v2, /device:TPU:1, one launch (start us, length us, event | category | flops | bytes accessed | tf_op | source)
XLA Modules:
  0.0 154.3 jit_solution(10809609195648411627)
XLA Ops:
  0.6 0.0 copy-start
  0.6 0.8 copy-done
  1.5 19.3 %all_to_all.20 = bf16[8,128,128]{2,1,0:T(8,128)(2,1)S(1)} all-to-all(bf16[8,128,128]{2,1,0:T(8,128)(2,1)S(1)} %broadcast_in_dim.10), channel_id=1, replica_groups=mesh['grid'=8,'y'=4,'xh'=2,'core'=2,'pts'=2] {'grid'}, dimensions={0} | all-to-all | bytes 524288 | tf_op jit(solution)/shard_map/all_to_all | solution.py:21
  20.8 2.6 %collective-permute-start.13 = (bf16[512,128]{1,0:T(8,128)(2,1)S(1)}, bf16[512,128]{1,0:T(8,128)(2,1)S(1)}, u32[]{:S(2)}, u32[]{:S(2)}) collective-permute-start(bf16[512,128]{1,0:T(8,128)(2,1)S(1)} %bitcast.51), channel_id=1, source_target_pairs={{0,5},{5,0},{1,4},{4,1},{2,7},{7,2},{3,6},{6,3},{8,13},{13,8},{9,1... | collective-permute-start | bytes 393224 | tf_op jit(solution)/shard_map/ppermute | solution.py:34
  23.4 0.5 collective-permute-start.14
  23.9 2.9 %collective-permute-start.4 = (bf16[512,128]{1,0:T(8,128)(2,1)S(1)}, bf16[512,128]{1,0:T(8,128)(2,1)S(1)}, u32[]{:S(2)}, u32[]{:S(2)}) collective-permute-start(bf16[512,128]{1,0:T(8,128)(2,1)S(1)} %bitcast.47), channel_id=1, source_target_pairs={{0,16},{8,24},{16,0},{24,8},{1,17},{9,25},{17,1},{25,9},{2,18},{10... | collective-permute-start | bytes 393224 | tf_op jit(solution)/shard_map/ppermute | solution.py:26
  26.8 0.4 collective-permute-start.5
  27.2 0.3 collective-permute-start.9
  27.5 1.3 collective-permute-done.14
  28.9 1.4 collective-permute-start.16
  30.2 0.0 collective-permute-done.4
  30.2 3.0 %collective-permute-done.5 = bf16[512,128]{1,0:T(8,128)(2,1)S(1)} collective-permute-done((bf16[512,128]{1,0:T(8,128)(2,1)S(1)}, bf16[512,128]{1,0:T(8,128)(2,1)S(1)}, u32[]{:S(2)}, u32[]{:S(2)}) %collective-permute-start.5) | collective-permute-done | bytes 131104 | tf_op jit(solution)/shard_map/ppermute | solution.py:26
  33.3 0.3 collective-permute-start.6
  33.6 0.0 collective-permute-start
  33.6 0.0 collective-permute-start.15
  33.7 2.5 %collective-permute-start.7 = (bf16[2,512,128]{2,1,0:T(8,128)(2,1)S(1)}, bf16[2,512,128]{2,1,0:T(8,128)(2,1)S(1)}, u32[]{:S(2)}, u32[]{:S(2)}) collective-permute-start(bf16[2,512,128]{2,1,0:T(8,128)(2,1)S(1)} %pad_maximum_fusion.1.refs_4_), channel_id=1, source_target_pairs={{0,5},{5,0},{1,4},{4,1},{2,7},{7,2},{3,6},{6,3},{8,13},{13,8},{9,1... | collective-permute-start | bytes 786440 | tf_op jit(solution)/shard_map/ppermute | solution.py:34
  36.3 1.2 collective-permute-done
  37.5 1.2 collective-permute-start.10
  38.7 2.6 %collective-permute-start.2 = (bf16[2,512,128]{2,1,0:T(8,128)(2,1)S(1)}, bf16[2,512,128]{2,1,0:T(8,128)(2,1)S(1)}, u32[]{:S(2)}, u32[]{:S(2)}) collective-permute-start(bf16[2,512,128]{2,1,0:T(8,128)(2,1)S(1)} %pad_maximum_fusion.refs_0_), channel_id=1, source_target_pairs={{0,5},{5,0},{1,4},{4,1},{2,7},{7,2},{3,6},{6,3},{8,13},{13,8},{9,1... | collective-permute-start | bytes 786440 | tf_op jit(solution)/shard_map/ppermute | solution.py:34
  41.3 0.5 collective-permute-start.12
  41.8 2.0 %broadcast_in_dim.11 = bf16[8,256,256]{2,1,0:T(8,128)(2,1)} broadcast(bf16[256,256]{1,0:T(8,128)(2,1)} %param.6), dimensions={1,2} | broadcast | bytes 1179648 | tf_op jit(solution)/shard_map/broadcast_in_dim | solution.py:264
  43.9 4.2 %all-to-all-start.1 = ((bf16[8,256,256]{2,1,0:T(8,128)(2,1)}), bf16[8,256,256]{2,1,0:T(8,128)(2,1)}, u32[]{:S(2)}, u32[]{:S(2)}) async-start(bf16[8,256,256]{2,1,0:T(8,128)(2,1)} %broadcast_in_dim.11), calls=%async_computation.1 | async-start | bytes 2097152 | tf_op jit(solution)/shard_map/all_to_all | solution.py:265
  48.1 0.1 collective-permute-start.1
  48.3 0.1 collective-permute-start.17
  48.4 0.8 collective-permute-start.8
  49.1 2.6 %collective-permute-start.11 = (bf16[2,512,128]{2,1,0:T(8,128)(2,1)S(1)}, bf16[2,512,128]{2,1,0:T(8,128)(2,1)}, u32[]{:S(2)}, u32[]{:S(2)}) collective-permute-start(bf16[2,512,128]{2,1,0:T(8,128)(2,1)S(1)} %collective-permute-done.10.refs_9_), channel_id=1, source_target_pairs={{0,24},{8,0},{16,8},{24,16},{1,25},{9,1},{17,9},{25,17},{2,26},{10... | collective-permute-start | bytes 786440 | tf_op jit(solution)/shard_map/ppermute | solution.py:26
  51.7 0.7 collective-permute-start.3
  52.5 0.1 pad_add_fusion.1.place_ref
  52.6 0.7 dynamic_slice.18
  53.3 0.8 fusion.9
  54.2 3.1 %collective-permute-done.17.refs_14_ = bf16[2,512,128]{2,1,0:T(8,128)(2,1)S(1)} collective-permute-done((bf16[2,512,128]{2,1,0:T(8,128)(2,1)S(1)}, bf16[2,512,128]{2,1,0:T(8,128)(2,1)S(1)}, u32[]{:S(2)}, u32[]{:S(2)}) %collective-permute-start.17) | collective-permute-done | bytes 262176 | tf_op jit(solution)/shard_map/ppermute | solution.py:26
  57.3 8.3 %pick.1 = (f32[256,1024]{1,0:T(8,128)S(1)}, f32[256,1024]{1,0:T(8,128)S(1)}, bf16[1024,1024]{1,0:T(8,128)(2,1)}, bf16[8,2048,128]{2,1,0:T(8,128)(2,1)}) custom-call(s32[1536]{0:T(1024)S(1)} %pad_add_fusion.spots_ref, s32[3]{0:T(128)S(1)} %pad_add_fusion.1.place_ref, bf16[2,512,128]{2,1,0:T(8,128)(2,1)S(1)} %pad_maximum_fusion.refs_0_, ...), custom_call_target="tpu_custom_call" | custom-call | flops 1073741824 | bytes 8388608 | tf_op jit(solution)/shard_map/pick/pallas_call | solution.py:134
  65.6 9.8 %collective-permute-start.18 = (f32[256,1024]{1,0:T(8,128)S(1)}, f32[256,1024]{1,0:T(8,128)S(1)}, u32[]{:S(2)}, u32[]{:S(2)}) collective-permute-start(f32[256,1024]{1,0:T(8,128)S(1)} %get-tuple-element.19), channel_id=1, source_target_pairs={{0,2},{2,0},{1,3},{3,1},{4,6},{6,4},{5,7},{7,5},{8,10},{10,8},{9,1... | collective-permute-start | bytes 3145736 | tf_op jit(solution)/shard_map/ppermute | solution.py:58
  75.4 2.3 %collective-permute-done.18 = f32[256,1024]{1,0:T(8,128)S(1)} collective-permute-done((f32[256,1024]{1,0:T(8,128)S(1)}, f32[256,1024]{1,0:T(8,128)S(1)}, u32[]{:S(2)}, u32[]{:S(2)}) %collective-permute-start.18) | collective-permute-done | bytes 1048608 | tf_op jit(solution)/shard_map/ppermute | solution.py:58
  77.7 0.3 multiply_convert_fusion.rows_ref
  77.9 0.5 collective-permute-start.19
  78.4 0.1 collective-permute-start.28
  78.5 0.8 own.1.own_ref
  79.3 0.6 collective-permute-done.19.other_ref
  79.9 0.9 applied.1
  80.9 1.6 %collective-permute-start.20 = (bf16[16,8,512]{2,1,0:T(8,128)(2,1)S(1)}, bf16[16,8,512]{2,1,0:T(8,128)(2,1)S(1)}, u32[]{:S(2)}, u32[]{:S(2)}) collective-permute-start(bf16[16,8,512]{2,1,0:T(8,128)(2,1)S(1)} %get-tuple-element.23), channel_id=1, source_target_pairs={{0,32},{32,64},{64,96},{96,128},{128,160},{160,192},{192,224},{224... | collective-permute-start | bytes 393224 | tf_op jit(solution)/shard_map/ppermute | solution.py:218
  82.5 2.1 %collective-permute-start.21 = (bf16[16,8,512]{2,1,0:T(8,128)(2,1)S(1)}, bf16[16,8,512]{2,1,0:T(8,128)(2,1)S(1)}, u32[]{:S(2)}, u32[]{:S(2)}) collective-permute-start(bf16[16,8,512]{2,1,0:T(8,128)(2,1)S(1)} %get-tuple-element.24), channel_id=1, source_target_pairs={{0,64},{32,96},{64,128},{96,160},{128,192},{160,224},{192,0},{224,... | collective-permute-start | bytes 393224 | tf_op jit(solution)/shard_map/ppermute | solution.py:218
  84.5 2.4 %collective-permute-start.22 = (bf16[8,8,512]{2,1,0:T(8,128)(2,1)S(1)}, bf16[8,8,512]{2,1,0:T(8,128)(2,1)S(1)}, u32[]{:S(2)}, u32[]{:S(2)}) collective-permute-start(bf16[8,8,512]{2,1,0:T(8,128)(2,1)S(1)} %get-tuple-element.25), channel_id=1, source_target_pairs={{0,96},{32,128},{64,160},{96,192},{128,224},{160,0},{192,32},{224,... | collective-permute-start | bytes 196616 | tf_op jit(solution)/shard_map/ppermute | solution.py:218
  87.0 2.4 %collective-permute-start.24 = (bf16[16,8,512]{2,1,0:T(8,128)(2,1)S(1)}, bf16[16,8,512]{2,1,0:T(8,128)(2,1)S(1)}, u32[]{:S(2)}, u32[]{:S(2)}) collective-permute-start(bf16[16,8,512]{2,1,0:T(8,128)(2,1)S(1)} %get-tuple-element.27), channel_id=1, source_target_pairs={{0,224},{32,0},{64,32},{96,64},{128,96},{160,128},{192,160},{224,1... | collective-permute-start | bytes 393224 | tf_op jit(solution)/shard_map/ppermute | solution.py:218
  89.4 7.8 %collective-permute-done.22 = bf16[8,8,512]{2,1,0:T(8,128)(2,1)S(1)} collective-permute-done((bf16[8,8,512]{2,1,0:T(8,128)(2,1)S(1)}, bf16[8,8,512]{2,1,0:T(8,128)(2,1)S(1)}, u32[]{:S(2)}, u32[]{:S(2)}) %collective-permute-start.22) | collective-permute-done | bytes 65568 | tf_op jit(solution)/shard_map/ppermute | solution.py:218
  97.1 4.7 %collective-permute-start.25 = (bf16[16,8,512]{2,1,0:T(8,128)(2,1)S(1)}, bf16[16,8,512]{2,1,0:T(8,128)(2,1)S(1)}, u32[]{:S(2)}, u32[]{:S(2)}) collective-permute-start(bf16[16,8,512]{2,1,0:T(8,128)(2,1)S(1)} %get-tuple-element.28), channel_id=1, source_target_pairs={{0,192},{32,224},{64,0},{96,32},{128,64},{160,96},{192,128},{224,1... | collective-permute-start | bytes 393224 | tf_op jit(solution)/shard_map/ppermute | solution.py:218
  101.8 0.1 add_convert_fusion.2
  101.9 1.3 collective-permute-start.23
  103.1 7.0 %collective-permute-done.26 = bf16[8,8,512]{2,1,0:T(8,128)(2,1)S(1)} collective-permute-done((bf16[8,8,512]{2,1,0:T(8,128)(2,1)S(1)}, bf16[8,8,512]{2,1,0:T(8,128)(2,1)S(1)}, u32[]{:S(2)}, u32[]{:S(2)}) %collective-permute-start.26) | collective-permute-done | bytes 65568 | tf_op jit(solution)/shard_map/ppermute | solution.py:218
  110.1 0.1 add_convert_fusion.1
  110.2 0.3 collective-permute-start.27
  110.5 3.8 %collective-permute-done.27 = bf16[16,8,512]{2,1,0:T(8,128)(2,1)S(1)} collective-permute-done((bf16[16,8,512]{2,1,0:T(8,128)(2,1)S(1)}, bf16[16,8,512]{2,1,0:T(8,128)(2,1)S(1)}, u32[]{:S(2)}, u32[]{:S(2)}) %collective-permute-start.27) | collective-permute-done | bytes 131104 | tf_op jit(solution)/shard_map/ppermute | solution.py:218
  114.3 0.1 fusion.2
  114.4 0.5 fusion.3
  114.8 1.7 %fusion.1 = bf16[16,8,2048]{2,1,0:T(8,128)(2,1)S(1)} fusion(f32[128,2048]{1,0:T(8,128)S(1)} %fusion.3, bf16[2048,256]{1,0:T(8,128)(2,1)} %bitcast.14, bf16[128,512]{1,0:T(8,128)(2,1)S(1)} %fusion.2), kind=kOutput, calls=%fused_computation.2 | convolution fusion | flops 134742016 | bytes 2686976 | tf_op jit(solution)/shard_map/dot_general | solution.py:287
  116.5 13.6 %all_to_all.21 = bf16[16,8,2048]{2,1,0:T(8,128)(2,1)S(1)} all-to-all(bf16[16,8,2048]{2,1,0:T(8,128)(2,1)S(1)} %fusion.1), channel_id=1, replica_groups=mesh['grid'=8,'y'=4,'xh'=2,'core'=2,'pts'=2] {'y','xh','pts'}, dimensions={0} | all-to-all | bytes 1048576 | tf_op jit(solution)/shard_map/all_to_all | solution.py:290
  130.1 0.1 convert_reduce_fusion
  130.2 3.3 %collective-permute-start.29 = (f32[8,2048]{1,0:T(8,128)S(1)}, f32[8,2048]{1,0:T(8,128)S(1)}, u32[]{:S(2)}, u32[]{:S(2)}) collective-permute-start(f32[8,2048]{1,0:T(8,128)S(1)} %get-tuple-element.37), channel_id=1, source_target_pairs={{0,2},{2,0},{1,3},{3,1},{4,6},{6,4},{5,7},{7,5},{8,10},{10,8},{9,1... | collective-permute-start | bytes 196616 | tf_op jit(solution)/shard_map/ppermute | solution.py:58
  133.5 0.9 collective-permute-done.29
  134.4 0.1 reshape.51
  134.6 0.1 constant_dynamic-slice_fusion
  134.7 2.8 %convolution_multiply_fusion = f32[16,8,128]{2,0,1:T(8,128)S(1)} fusion(bf16[8,2048,128]{2,1,0:T(8,128)(2,1)} %get-tuple-element.31, f32[2,8,2048]{2,1,0:T(8,128)S(1)} %reverse_select_fusion), kind=kOutput, calls=%fused_computation.3 | convolution fusion | flops 67158016 | bytes 4390912 | tf_op jit(solution)/shard_map/dot_general | solution.py:296
  137.5 16.2 %all_to_all.22 = f32[16,2,8,128]{3,2,1,0:T(8,128)S(1)} all-to-all(f32[16,2,8,128]{3,2,1,0:T(8,128)S(1)} %copy.8), channel_id=1, replica_groups=mesh['grid'=8,'y'=4,'xh'=2,'core'=2,'pts'=2] {'grid','core'}, dimensions={0} | all-to-all | bytes 262144 | tf_op jit(solution)/shard_map/all_to_all | solution.py:303
  153.7 0.7 slice_bitcast_fusion
  (39 shorter events, 0.3 us)
Async XLA Ops:
  0.6 0.8 copy-start
  20.8 6.7 %collective-permute-start.13 = (bf16[512,128]{1,0:T(8,128)(2,1)S(1)}, bf16[512,128]{1,0:T(8,128)(2,1)S(1)}, u32[]{:S(2)}, u32[]{:S(2)}) collective-permute-start(bf16[512,128]{1,0:T(8,128)(2,1)S(1)} %bitcast.51), channel_id=1, source_target_pairs={{0,5},{5,0},{1,4},{4,1},{2,7},{7,2},{3,6},{6,3},{8,13},{13,8},{9,1... | collective-permute-start | bytes 393224 | tf_op jit(solution)/shard_map/ppermute | solution.py:34
  23.4 5.4 %collective-permute-start.14 = (bf16[512,128]{1,0:T(8,128)(2,1)S(1)}, bf16[512,128]{1,0:T(8,128)(2,1)S(1)}, u32[]{:S(2)}, u32[]{:S(2)}) collective-permute-start(bf16[512,128]{1,0:T(8,128)(2,1)S(1)} %bitcast.52), channel_id=1, source_target_pairs={{0,4},{4,0},{1,5},{5,1},{2,6},{6,2},{3,7},{7,3},{8,12},{12,8},{9,1... | collective-permute-start | bytes 393224 | tf_op jit(solution)/shard_map/ppermute | solution.py:38
  23.9 6.3 %collective-permute-start.4 = (bf16[512,128]{1,0:T(8,128)(2,1)S(1)}, bf16[512,128]{1,0:T(8,128)(2,1)S(1)}, u32[]{:S(2)}, u32[]{:S(2)}) collective-permute-start(bf16[512,128]{1,0:T(8,128)(2,1)S(1)} %bitcast.47), channel_id=1, source_target_pairs={{0,16},{8,24},{16,0},{24,8},{1,17},{9,25},{17,1},{25,9},{2,18},{10... | collective-permute-start | bytes 393224 | tf_op jit(solution)/shard_map/ppermute | solution.py:26
  26.8 6.4 %collective-permute-start.5 = (bf16[512,128]{1,0:T(8,128)(2,1)S(1)}, bf16[512,128]{1,0:T(8,128)(2,1)S(1)}, u32[]{:S(2)}, u32[]{:S(2)}) collective-permute-start(bf16[512,128]{1,0:T(8,128)(2,1)S(1)} %bitcast.48), channel_id=1, source_target_pairs={{0,8},{8,16},{16,24},{24,0},{1,9},{9,17},{17,25},{25,1},{2,10},{10... | collective-permute-start | bytes 393224 | tf_op jit(solution)/shard_map/ppermute | solution.py:26
  27.2 6.5 %collective-permute-start.9 = (bf16[512,128]{1,0:T(8,128)(2,1)S(1)}, bf16[512,128]{1,0:T(8,128)(2,1)S(1)}, u32[]{:S(2)}, u32[]{:S(2)}) collective-permute-start(bf16[512,128]{1,0:T(8,128)(2,1)S(1)} %bitcast.53), channel_id=1, source_target_pairs={{0,1},{1,0},{4,5},{5,4},{2,3},{3,2},{6,7},{7,6},{8,9},{9,8},{12,13... | collective-permute-start | bytes 393224 | tf_op jit(solution)/shard_map/ppermute | solution.py:30
  28.9 9.9 %collective-permute-start.16 = (bf16[2,512,128]{2,1,0:T(8,128)(2,1)S(1)}, bf16[2,512,128]{2,1,0:T(8,128)(2,1)S(1)}, u32[]{:S(2)}, u32[]{:S(2)}) collective-permute-start(bf16[2,512,128]{2,1,0:T(8,128)(2,1)S(1)} %pad_maximum_fusion.3.refs_12_), channel_id=1, source_target_pairs={{0,8},{8,16},{16,24},{24,0},{1,9},{9,17},{17,25},{25,1},{2,10},{10... | collective-permute-start | bytes 786440 | tf_op jit(solution)/shard_map/ppermute | solution.py:26
  33.3 8.0 %collective-permute-start.6 = (bf16[2,512,128]{2,1,0:T(8,128)(2,1)S(1)}, bf16[2,512,128]{2,1,0:T(8,128)(2,1)S(1)}, u32[]{:S(2)}, u32[]{:S(2)}) collective-permute-start(bf16[2,512,128]{2,1,0:T(8,128)(2,1)S(1)} %pad_maximum_fusion.1.refs_4_), channel_id=1, source_target_pairs={{0,1},{1,0},{4,5},{5,4},{2,3},{3,2},{6,7},{7,6},{8,9},{9,8},{12,13... | collective-permute-start | bytes 786440 | tf_op jit(solution)/shard_map/ppermute | solution.py:30
  33.6 3.8 %collective-permute-start = (bf16[512,128]{1,0:T(8,128)(2,1)S(1)}, bf16[512,128]{1,0:T(8,128)(2,1)S(1)}, u32[]{:S(2)}, u32[]{:S(2)}) collective-permute-start(bf16[512,128]{1,0:T(8,128)(2,1)S(1)} %bitcast.49), channel_id=1, source_target_pairs={{0,24},{8,0},{16,8},{24,16},{1,25},{9,1},{17,9},{25,17},{2,26},{10... | collective-permute-start | bytes 393224 | tf_op jit(solution)/shard_map/ppermute | solution.py:26
  33.6 14.5 %collective-permute-start.15 = (bf16[2,512,128]{2,1,0:T(8,128)(2,1)S(1)}, bf16[2,512,128]{2,1,0:T(8,128)(2,1)S(1)}, u32[]{:S(2)}, u32[]{:S(2)}) collective-permute-start(bf16[2,512,128]{2,1,0:T(8,128)(2,1)S(1)} %pad_maximum_fusion.3.refs_12_), channel_id=1, source_target_pairs={{0,24},{8,0},{16,8},{24,16},{1,25},{9,1},{17,9},{25,17},{2,26},{10... | collective-permute-start | bytes 786440 | tf_op jit(solution)/shard_map/ppermute | solution.py:26
  33.7 14.6 %collective-permute-start.7 = (bf16[2,512,128]{2,1,0:T(8,128)(2,1)S(1)}, bf16[2,512,128]{2,1,0:T(8,128)(2,1)S(1)}, u32[]{:S(2)}, u32[]{:S(2)}) collective-permute-start(bf16[2,512,128]{2,1,0:T(8,128)(2,1)S(1)} %pad_maximum_fusion.1.refs_4_), channel_id=1, source_target_pairs={{0,5},{5,0},{1,4},{4,1},{2,7},{7,2},{3,6},{6,3},{8,13},{13,8},{9,1... | collective-permute-start | bytes 786440 | tf_op jit(solution)/shard_map/ppermute | solution.py:34
  37.5 10.9 %collective-permute-start.10 = (bf16[2,512,128]{2,1,0:T(8,128)(2,1)S(1)}, bf16[2,512,128]{2,1,0:T(8,128)(2,1)S(1)}, u32[]{:S(2)}, u32[]{:S(2)}) collective-permute-start(bf16[2,512,128]{2,1,0:T(8,128)(2,1)S(1)} %pad_maximum_fusion.2.refs_8_), channel_id=1, source_target_pairs={{0,24},{8,0},{16,8},{24,16},{1,25},{9,1},{17,9},{25,17},{2,26},{10... | collective-permute-start | bytes 786440 | tf_op jit(solution)/shard_map/ppermute | solution.py:26
  38.7 10.4 %collective-permute-start.2 = (bf16[2,512,128]{2,1,0:T(8,128)(2,1)S(1)}, bf16[2,512,128]{2,1,0:T(8,128)(2,1)S(1)}, u32[]{:S(2)}, u32[]{:S(2)}) collective-permute-start(bf16[2,512,128]{2,1,0:T(8,128)(2,1)S(1)} %pad_maximum_fusion.refs_0_), channel_id=1, source_target_pairs={{0,5},{5,0},{1,4},{4,1},{2,7},{7,2},{3,6},{6,3},{8,13},{13,8},{9,1... | collective-permute-start | bytes 786440 | tf_op jit(solution)/shard_map/ppermute | solution.py:34
  41.3 10.4 %collective-permute-start.12 = (bf16[2,512,128]{2,1,0:T(8,128)(2,1)S(1)}, bf16[2,512,128]{2,1,0:T(8,128)(2,1)S(1)}, u32[]{:S(2)}, u32[]{:S(2)}) collective-permute-start(bf16[2,512,128]{2,1,0:T(8,128)(2,1)S(1)} %pad_maximum_fusion.2.refs_8_), channel_id=1, source_target_pairs={{0,8},{8,16},{16,24},{24,0},{1,9},{9,17},{17,25},{25,1},{2,10},{10... | collective-permute-start | bytes 786440 | tf_op jit(solution)/shard_map/ppermute | solution.py:26
  43.9 34.5 %all-to-all-start.1 = ((bf16[8,256,256]{2,1,0:T(8,128)(2,1)}), bf16[8,256,256]{2,1,0:T(8,128)(2,1)}, u32[]{:S(2)}, u32[]{:S(2)}) async-start(bf16[8,256,256]{2,1,0:T(8,128)(2,1)} %broadcast_in_dim.11), calls=%async_computation.1 | async-start | bytes 2097152 | tf_op jit(solution)/shard_map/all_to_all | solution.py:265
  48.1 6.0 %collective-permute-start.1 = (bf16[2,512,128]{2,1,0:T(8,128)(2,1)S(1)}, bf16[2,512,128]{2,1,0:T(8,128)(2,1)S(1)}, u32[]{:S(2)}, u32[]{:S(2)}) collective-permute-start(bf16[2,512,128]{2,1,0:T(8,128)(2,1)S(1)} %pad_maximum_fusion.refs_0_), channel_id=1, source_target_pairs={{0,1},{1,0},{4,5},{5,4},{2,3},{3,2},{6,7},{7,6},{8,9},{9,8},{12,13... | collective-permute-start | bytes 786440 | tf_op jit(solution)/shard_map/ppermute | solution.py:30
  48.3 9.0 %collective-permute-start.17 = (bf16[2,512,128]{2,1,0:T(8,128)(2,1)S(1)}, bf16[2,512,128]{2,1,0:T(8,128)(2,1)S(1)}, u32[]{:S(2)}, u32[]{:S(2)}) collective-permute-start(bf16[2,512,128]{2,1,0:T(8,128)(2,1)S(1)} %collective-permute-done.16.refs_15_), channel_id=1, source_target_pairs={{0,8},{8,16},{16,24},{24,0},{1,9},{9,17},{17,25},{25,1},{2,10},{10... | collective-permute-start | bytes 786440 | tf_op jit(solution)/shard_map/ppermute | solution.py:26
  48.4 8.9 %collective-permute-start.8 = (bf16[2,512,128]{2,1,0:T(8,128)(2,1)S(1)}, bf16[2,512,128]{2,1,0:T(8,128)(2,1)}, u32[]{:S(2)}, u32[]{:S(2)}) collective-permute-start(bf16[2,512,128]{2,1,0:T(8,128)(2,1)S(1)} %collective-permute-done.6.refs_5_), channel_id=1, source_target_pairs={{0,5},{5,0},{1,4},{4,1},{2,7},{7,2},{3,6},{6,3},{8,13},{13,8},{9,1... | collective-permute-start | bytes 786440 | tf_op jit(solution)/shard_map/ppermute | solution.py:34
  49.1 8.1 %collective-permute-start.11 = (bf16[2,512,128]{2,1,0:T(8,128)(2,1)S(1)}, bf16[2,512,128]{2,1,0:T(8,128)(2,1)}, u32[]{:S(2)}, u32[]{:S(2)}) collective-permute-start(bf16[2,512,128]{2,1,0:T(8,128)(2,1)S(1)} %collective-permute-done.10.refs_9_), channel_id=1, source_target_pairs={{0,24},{8,0},{16,8},{24,16},{1,25},{9,1},{17,9},{25,17},{2,26},{10... | collective-permute-start | bytes 786440 | tf_op jit(solution)/shard_map/ppermute | solution.py:26
  51.7 5.6 %collective-permute-start.3 = (bf16[2,512,128]{2,1,0:T(8,128)(2,1)S(1)}, bf16[2,512,128]{2,1,0:T(8,128)(2,1)}, u32[]{:S(2)}, u32[]{:S(2)}) collective-permute-start(bf16[2,512,128]{2,1,0:T(8,128)(2,1)S(1)} %collective-permute-done.2.refs_2_), channel_id=1, source_target_pairs={{0,1},{1,0},{4,5},{5,4},{2,3},{3,2},{6,7},{7,6},{8,9},{9,8},{12,13... | collective-permute-start | bytes 786440 | tf_op jit(solution)/shard_map/ppermute | solution.py:30
  52.5 25.1 %copy-start.2 = (bf16[256,1024]{1,0:T(8,128)(2,1)S(1)}, bf16[256,1024]{1,0:T(8,128)(2,1)}, u32[]{:S(2)}) copy-start(bf16[256,1024]{1,0:T(8,128)(2,1)} %param.7) | copy-start | bytes 1572868
  65.6 13.0 %copy-start.1 = (bf16[1024,1024]{1,0:T(8,128)(2,1)S(1)}, bf16[1024,1024]{1,0:T(8,128)(2,1)}, u32[]{:S(2)}) copy-start(bf16[1024,1024]{1,0:T(8,128)(2,1)} %get-tuple-element.17.picked_ref) | copy-start | bytes 6291460
  65.6 12.1 %collective-permute-start.18 = (f32[256,1024]{1,0:T(8,128)S(1)}, f32[256,1024]{1,0:T(8,128)S(1)}, u32[]{:S(2)}, u32[]{:S(2)}) collective-permute-start(f32[256,1024]{1,0:T(8,128)S(1)} %get-tuple-element.19), channel_id=1, source_target_pairs={{0,2},{2,0},{1,3},{3,1},{4,6},{6,4},{5,7},{7,5},{8,10},{10,8},{9,1... | collective-permute-start | bytes 3145736 | tf_op jit(solution)/shard_map/ppermute | solution.py:58
  77.9 2.0 %collective-permute-start.19 = (bf16[256,1024]{1,0:T(8,128)(2,1)S(1)}, bf16[256,1024]{1,0:T(8,128)(2,1)S(1)}, u32[]{:S(2)}, u32[]{:S(2)}) collective-permute-start(bf16[256,1024]{1,0:T(8,128)(2,1)S(1)} %multiply_convert_fusion.rows_ref), channel_id=1, source_target_pairs={{0,2},{2,0},{1,3},{3,1},{4,6},{6,4},{5,7},{7,5},{8,10},{10,8},{9,1... | collective-permute-start | bytes 1572872 | tf_op jit(solution)/shard_map/ppermute | solution.py:58
  78.4 35.9 %collective-permute-start.28 = (bf16[2048,256]{1,0:T(8,128)(2,1)}, bf16[2048,256]{1,0:T(8,128)(2,1)S(1)}, u32[]{:S(2)}, u32[]{:S(2)}) collective-permute-start(bf16[2048,256]{1,0:T(8,128)(2,1)} %bitcast.14), channel_id=1, source_target_pairs={{0,2},{2,0},{1,3},{3,1},{4,6},{6,4},{5,7},{7,5},{8,10},{10,8},{9,1... | collective-permute-start | bytes 3145736 | tf_op jit(solution)/shard_map/ppermute | solution.py:58
  80.9 21.0 %collective-permute-start.20 = (bf16[16,8,512]{2,1,0:T(8,128)(2,1)S(1)}, bf16[16,8,512]{2,1,0:T(8,128)(2,1)S(1)}, u32[]{:S(2)}, u32[]{:S(2)}) collective-permute-start(bf16[16,8,512]{2,1,0:T(8,128)(2,1)S(1)} %get-tuple-element.23), channel_id=1, source_target_pairs={{0,32},{32,64},{64,96},{96,128},{128,160},{160,192},{192,224},{224... | collective-permute-start | bytes 393224 | tf_op jit(solution)/shard_map/ppermute | solution.py:218
  82.5 19.4 %collective-permute-start.21 = (bf16[16,8,512]{2,1,0:T(8,128)(2,1)S(1)}, bf16[16,8,512]{2,1,0:T(8,128)(2,1)S(1)}, u32[]{:S(2)}, u32[]{:S(2)}) collective-permute-start(bf16[16,8,512]{2,1,0:T(8,128)(2,1)S(1)} %get-tuple-element.24), channel_id=1, source_target_pairs={{0,64},{32,96},{64,128},{96,160},{128,192},{160,224},{192,0},{224,... | collective-permute-start | bytes 393224 | tf_op jit(solution)/shard_map/ppermute | solution.py:218
  84.5 12.6 %collective-permute-start.22 = (bf16[8,8,512]{2,1,0:T(8,128)(2,1)S(1)}, bf16[8,8,512]{2,1,0:T(8,128)(2,1)S(1)}, u32[]{:S(2)}, u32[]{:S(2)}) collective-permute-start(bf16[8,8,512]{2,1,0:T(8,128)(2,1)S(1)} %get-tuple-element.25), channel_id=1, source_target_pairs={{0,96},{32,128},{64,160},{96,192},{128,224},{160,0},{192,32},{224,... | collective-permute-start | bytes 196616 | tf_op jit(solution)/shard_map/ppermute | solution.py:218
  87.0 23.1 %collective-permute-start.24 = (bf16[16,8,512]{2,1,0:T(8,128)(2,1)S(1)}, bf16[16,8,512]{2,1,0:T(8,128)(2,1)S(1)}, u32[]{:S(2)}, u32[]{:S(2)}) collective-permute-start(bf16[16,8,512]{2,1,0:T(8,128)(2,1)S(1)} %get-tuple-element.27), channel_id=1, source_target_pairs={{0,224},{32,0},{64,32},{96,64},{128,96},{160,128},{192,160},{224,1... | collective-permute-start | bytes 393224 | tf_op jit(solution)/shard_map/ppermute | solution.py:218
  97.1 13.0 %collective-permute-start.25 = (bf16[16,8,512]{2,1,0:T(8,128)(2,1)S(1)}, bf16[16,8,512]{2,1,0:T(8,128)(2,1)S(1)}, u32[]{:S(2)}, u32[]{:S(2)}) collective-permute-start(bf16[16,8,512]{2,1,0:T(8,128)(2,1)S(1)} %get-tuple-element.28), channel_id=1, source_target_pairs={{0,192},{32,224},{64,0},{96,32},{128,64},{160,96},{192,128},{224,1... | collective-permute-start | bytes 393224 | tf_op jit(solution)/shard_map/ppermute | solution.py:218
  101.8 8.3 %collective-permute-start.26 = (bf16[8,8,512]{2,1,0:T(8,128)(2,1)S(1)}, bf16[8,8,512]{2,1,0:T(8,128)(2,1)S(1)}, u32[]{:S(2)}, u32[]{:S(2)}) collective-permute-start(bf16[8,8,512]{2,1,0:T(8,128)(2,1)S(1)} %get-tuple-element.29), channel_id=1, source_target_pairs={{0,160},{32,192},{64,224},{96,0},{128,32},{160,64},{192,96},{224,1... | collective-permute-start | bytes 196616 | tf_op jit(solution)/shard_map/ppermute | solution.py:218
  101.9 8.6 %collective-permute-start.23 = (bf16[16,8,512]{2,1,0:T(8,128)(2,1)S(1)}, bf16[16,8,512]{2,1,0:T(8,128)(2,1)S(1)}, u32[]{:S(2)}, u32[]{:S(2)}) collective-permute-start(bf16[16,8,512]{2,1,0:T(8,128)(2,1)S(1)} %add_convert_fusion.2), channel_id=1, source_target_pairs={{0,32},{32,64},{64,96},{96,128},{128,160},{160,192},{192,224},{224... | collective-permute-start | bytes 393224 | tf_op jit(solution)/shard_map/ppermute | solution.py:218
  110.2 4.1 %collective-permute-start.27 = (bf16[16,8,512]{2,1,0:T(8,128)(2,1)S(1)}, bf16[16,8,512]{2,1,0:T(8,128)(2,1)S(1)}, u32[]{:S(2)}, u32[]{:S(2)}) collective-permute-start(bf16[16,8,512]{2,1,0:T(8,128)(2,1)S(1)} %add_convert_fusion.1), channel_id=1, source_target_pairs={{0,224},{32,0},{64,32},{96,64},{128,96},{160,128},{192,160},{224,1... | collective-permute-start | bytes 393224 | tf_op jit(solution)/shard_map/ppermute | solution.py:218
  130.2 4.2 %collective-permute-start.29 = (f32[8,2048]{1,0:T(8,128)S(1)}, f32[8,2048]{1,0:T(8,128)S(1)}, u32[]{:S(2)}, u32[]{:S(2)}) collective-permute-start(f32[8,2048]{1,0:T(8,128)S(1)} %get-tuple-element.37), channel_id=1, source_target_pairs={{0,2},{2,0},{1,3},{3,1},{4,6},{6,4},{5,7},{7,5},{8,10},{10,8},{9,1... | collective-permute-start | bytes 196616 | tf_op jit(solution)/shard_map/ppermute | solution.py:58
